TPU v7x, 32 devices: a 4x4x1 block of a 4x4x8 slice. The times are simulated.
32 devices in a mesh: data: 1 (over z), tensor: 32 (over y, x, core).
Axes of the slice: x: 4, y: 4, z: 1, core: 2. Of those that a mesh axis runs over, the one named last changes fastest.
The devices are a block of a 4x4x8 slice.
Arguments:
- x: bfloat16 [8, 1024, 4096], P('data')
- adapter_ids: int32 [8], P('data')
- norm_gain: float32 [4096], replicated
- w_query: bfloat16 [4096, 32, 128], P(None, 'tensor')
- w_key: bfloat16 [4096, 32, 128], P(None, 'tensor')
- w_value: bfloat16 [4096, 32, 128], P(None, 'tensor')
- w_out: bfloat16 [32, 128, 4096], P('tensor')
- w_gate: bfloat16 [4096, 16384], P(None, 'tensor')
- w_up: bfloat16 [4096, 16384], P(None, 'tensor')
- w_down: bfloat16 [16384, 4096], P('tensor')
- lora_a_query: bfloat16 [2, 4096, 128], P(None, None, 'tensor')
- lora_b_query: bfloat16 [2, 128, 32, 128], P(None, None, 'tensor')
- lora_a_key: bfloat16 [2, 4096, 128], P(None, None, 'tensor')
- lora_b_key: bfloat16 [2, 128, 32, 128], P(None, None, 'tensor')
- lora_a_value: bfloat16 [2, 4096, 128], P(None, None, 'tensor')
- lora_b_value: bfloat16 [2, 128, 32, 128], P(None, None, 'tensor')
- lora_a_out: bfloat16 [2, 32, 128, 128], P(None, 'tensor')
- lora_b_out: bfloat16 [2, 128, 4096], P(None, None, 'tensor')
- lora_a_gate: bfloat16 [2, 4096, 128], P(None, None, 'tensor')
- lora_b_gate: bfloat16 [2, 128, 16384], P(None, None, 'tensor')
- lora_a_up: bfloat16 [2, 4096, 128], P(None, None, 'tensor')
- lora_b_up: bfloat16 [2, 128, 16384], P(None, None, 'tensor')
- lora_a_down: bfloat16 [2, 16384, 128], P(None, 'tensor')
- lora_b_down: bfloat16 [2, 128, 4096], P(None, None, 'tensor')
Outputs:
- output: bfloat16 [8, 1024, 4096], P('data')
All inputs are finite; a program needn't handle non-finite values.
Results may differ from a plain program's by a relative error of at most 0.013888.
Values are sent between devices in bfloat16 or wider.
A program may use at most 768 MiB of HBM per device.

v0:
```python
import jax
import jax.numpy as jnp
import math
from jax import lax
from jax.sharding import PartitionSpec as P

ALPHA = 16
EPS = 1e-5
ROPE_BASE = 10000.0


def rms_norm(x_blk, norm_gain):
    x_f32 = x_blk.astype(jnp.float32)
    return (x_f32 * lax.rsqrt(jnp.mean(x_f32 * x_f32, axis=-1, keepdims=True) + EPS) * norm_gain).astype(jnp.bfloat16)


def rope_tables(seq_len, head_dim):
    half_dim = head_dim // 2
    inv_freq = ROPE_BASE ** (-jnp.arange(half_dim, dtype=jnp.float32) / half_dim)
    angles = jnp.arange(seq_len, dtype=jnp.float32)[:, None] * inv_freq[None, :]
    return jnp.cos(angles)[:, None, :], jnp.sin(angles)[:, None, :]


def rope_rotate(vals, cos_t, sin_t):
    half_dim = vals.shape[-1] // 2
    first = vals[..., :half_dim]
    second = vals[..., half_dim:]
    return jnp.concatenate([first * cos_t - second * sin_t, second * cos_t + first * sin_t], axis=-1)


def causal_attention(query_rot, key_rot, value_heads):
    seq_len = query_rot.shape[1]
    head_dim = query_rot.shape[3]
    scores = jnp.einsum('bqhd,bkhd->bhqk', query_rot, key_rot, preferred_element_type=jnp.float32) / math.sqrt(head_dim)
    causal = jnp.arange(seq_len)[:, None] >= jnp.arange(seq_len)[None, :]
    probs_bf = jax.nn.softmax(jnp.where(causal, scores, -1e30), axis=-1).astype(jnp.bfloat16)
    return jnp.einsum('bhqk,bkhd->bqhd', probs_bf, value_heads, preferred_element_type=jnp.float32).astype(jnp.bfloat16)


def solution(mesh):
    batch_spec = P('data', None, None)
    head_cols = P(None, 'tensor', None)
    head_rows = P('tensor', None, None)
    ff_cols = P(None, 'tensor')
    ff_rows = P('tensor', None)
    last_split = P(None, None, 'tensor')
    b_heads = P(None, None, 'tensor', None)
    a_heads = P(None, 'tensor', None, None)
    in_specs = (batch_spec, P('data'), P(None), head_cols, head_cols, head_cols, head_rows, ff_cols, ff_cols, ff_rows, last_split, b_heads, last_split, b_heads, last_split, b_heads, a_heads, last_split, last_split, last_split, last_split, last_split, head_cols, last_split)

    def local_layer(x_blk, adapter_ids, norm_gain, w_query, w_key, w_value, w_out, w_gate, w_up, w_down, a_query, b_query, a_key, b_key, a_value, b_value, a_out, b_out, a_gate, b_gate, a_up, b_up, a_down, b_down):
        seq_len = x_blk.shape[1]
        rank = a_out.shape[-1]
        scale = ALPHA / rank
        normed = rms_norm(x_blk, norm_gain)
        cos_t, sin_t = rope_tables(seq_len, w_query.shape[-1])

        def gather_mid(a_stack):
            part_mid = jnp.einsum('bsd,bdr->bsr', normed, a_stack[adapter_ids], preferred_element_type=jnp.float32).astype(jnp.bfloat16)
            return lax.all_gather(part_mid, 'tensor', axis=2, tiled=True)

        def head_proj(weight, a_stack, b_stack):
            value_a8 = gather_mid(a_stack)
            base_out = jnp.einsum('bsd,dhe->bshe', normed, weight, preferred_element_type=jnp.float32)
            array_b8 = jnp.einsum('bsr,brhe->bshe', value_a8, b_stack[adapter_ids], preferred_element_type=jnp.float32)
            return base_out + scale * array_b8

        def ffn_proj(weight, a_stack, b_stack):
            value_a8 = gather_mid(a_stack)
            base_out = jnp.einsum('bsd,df->bsf', normed, weight, preferred_element_type=jnp.float32)
            array_b8 = jnp.einsum('bsr,brf->bsf', value_a8, b_stack[adapter_ids], preferred_element_type=jnp.float32)
            return base_out + scale * array_b8

        query_rot = rope_rotate(head_proj(w_query, a_query, b_query), cos_t, sin_t).astype(jnp.bfloat16)
        key_rot = rope_rotate(head_proj(w_key, a_key, b_key), cos_t, sin_t).astype(jnp.bfloat16)
        value_heads = head_proj(w_value, a_value, b_value).astype(jnp.bfloat16)
        attended = causal_attention(query_rot, key_rot, value_heads)
        mlp_mixed = (jax.nn.silu(ffn_proj(w_gate, a_gate, b_gate)) * ffn_proj(w_up, a_up, b_up)).astype(jnp.bfloat16)
        mid_out = lax.psum(jnp.einsum('bshe,bher->bsr', attended, a_out[adapter_ids], preferred_element_type=jnp.float32).astype(jnp.bfloat16), 'tensor')
        mid_down = lax.psum(jnp.einsum('bsf,bfr->bsr', mlp_mixed, a_down[adapter_ids], preferred_element_type=jnp.float32).astype(jnp.bfloat16), 'tensor')
        base_part = (jnp.einsum('bshe,hed->bsd', attended, w_out, preferred_element_type=jnp.float32) + jnp.einsum('bsf,fd->bsd', mlp_mixed, w_down, preferred_element_type=jnp.float32)).astype(jnp.bfloat16)
        base_sum = lax.psum_scatter(base_part, 'tensor', scatter_dimension=2, tiled=True)
        local_c8 = jnp.einsum('bsr,brd->bsd', mid_out, b_out[adapter_ids], preferred_element_type=jnp.float32) + jnp.einsum('bsr,brd->bsd', mid_down, b_down[adapter_ids], preferred_element_type=jnp.float32)
        share_width = base_sum.shape[2]
        x_share = lax.dynamic_slice_in_dim(x_blk, lax.axis_index('tensor') * share_width, share_width, axis=2)
        y_share = (x_share.astype(jnp.float32) + base_sum.astype(jnp.float32) + scale * local_c8).astype(jnp.bfloat16)
        return lax.all_gather(y_share, 'tensor', axis=2, tiled=True)

    return jax.shard_map(local_layer, mesh=mesh, in_specs=in_specs, out_specs=batch_spec, check_vma=False)
```

profile of v0, /device:TPU:97, one launch (start us, length us, event | category | flops | bytes accessed | tf_op | source)
XLA Modules:
  0.0 1186.8 jit_solution(10093035138167076755)
XLA Ops:
  7.3 20.9 %fusion.1 = f32[8,1024]{1,0:T(8,128)S(1)} fusion(bf16[8,1024,4096]{2,1,0:T(8,128)(2,1)} %param.24), kind=kLoop, calls=%fused_computation.17 | loop fusion | flops 100655104 | bytes 67141632 | tf_op jit(solution)/shard_map/reduce_sum | solution.py:14
  29.1 25.7 %fusion.65 = bf16[8,1024,4]{1,2,0:T(4,128)(2,1)S(1)} fusion(bf16[8,4096,4]{1,2,0:T(4,128)(2,1)S(1)} %gather_fusion.8, bf16[8,1024,4096]{2,1,0:T(8,128)(2,1)} %param.24, f32[4096]{0:T(1024)S(1)} %copy-done.26, f32[8,1024]{1,0:T(8,128)S(1)} %add_rsqrt_fusion), kind=kOutput, calls=%fused_computation.93 | convolution fusion | flops 402653184 | bytes 67485696 | tf_op jit(solution)/shard_map/bsd,bdr->bsr/dot_general | solution.py:59
  56.4 25.7 %fusion.68 = bf16[8,1024,4]{1,2,0:T(4,128)(2,1)S(1)} fusion(bf16[8,4096,4]{1,2,0:T(4,128)(2,1)S(1)} %gather_fusion.6, bf16[8,1024,4096]{2,1,0:T(8,128)(2,1)} %param.24, f32[4096]{0:T(1024)S(1)} %copy-done.26, f32[8,1024]{1,0:T(8,128)S(1)} %add_rsqrt_fusion), kind=kOutput, calls=%fused_computation.94 | convolution fusion | flops 402653184 | bytes 67485696 | tf_op jit(solution)/shard_map/bsd,bdr->bsr/dot_general | solution.py:59
  83.8 25.7 %fusion.74 = bf16[8,1024,4]{1,2,0:T(4,128)(2,1)S(1)} fusion(bf16[8,4096,4]{1,2,0:T(4,128)(2,1)S(1)} %gather_fusion.2, bf16[8,1024,4096]{2,1,0:T(8,128)(2,1)} %param.24, f32[4096]{0:T(1024)S(1)} %copy-done.26, f32[8,1024]{1,0:T(8,128)S(1)} %add_rsqrt_fusion), kind=kOutput, calls=%fused_computation.96 | convolution fusion | flops 402653184 | bytes 67485696 | tf_op jit(solution)/shard_map/bsd,bdr->bsr/dot_general | solution.py:59
  111.6 25.7 %fusion.71 = bf16[8,1024,4]{1,2,0:T(4,128)(2,1)S(1)} fusion(bf16[8,4096,4]{1,2,0:T(4,128)(2,1)S(1)} %gather_fusion.4, bf16[8,1024,4096]{2,1,0:T(8,128)(2,1)} %param.24, f32[4096]{0:T(1024)S(1)} %copy-done.26, f32[8,1024]{1,0:T(8,128)S(1)} %add_rsqrt_fusion), kind=kOutput, calls=%fused_computation.95 | convolution fusion | flops 402653184 | bytes 67485696 | tf_op jit(solution)/shard_map/bsd,bdr->bsr/dot_general | solution.py:59
  138.9 25.8 %fusion.77 = bf16[8,1024,4]{1,2,0:T(4,128)(2,1)S(1)} fusion(bf16[8,4096,4]{1,2,0:T(4,128)(2,1)S(1)} %gather_fusion, bf16[8,1024,4096]{2,1,0:T(8,128)(2,1)} %param.24, f32[4096]{0:T(1024)S(1)} %copy-done.26, f32[8,1024]{1,0:T(8,128)S(1)} %add_rsqrt_fusion), kind=kOutput, calls=%fused_computation.97 | convolution fusion | flops 402653184 | bytes 67485696 | tf_op jit(solution)/shard_map/bsd,bdr->bsr/dot_general | solution.py:59
  168.3 30.0 %fusion.45 = f32[8,1024,128]{1,2,0:T(8,128)} fusion(bf16[4096,1,128]{2,0,1:T(8,128)(2,1)S(1)} %copy-done.24, bf16[8,1024,4096]{2,1,0:T(8,128)(2,1)} %param.24, f32[4096]{0:T(1024)S(1)} %copy-done.26, f32[8,1024]{1,0:T(8,128)S(1)} %add_rsqrt_fusion), kind=kOutput, calls=%fused_computation.69 | convolution fusion | flops 8724152320 | bytes 72400896 | tf_op jit(solution)/shard_map/bsd,dhe->bshe/dot_general | solution.py:64
  199.6 32.0 %fusion.42 = f32[8,1024,128]{1,2,0:T(8,128)} fusion(bf16[4096,1,128]{2,0,1:T(8,128)(2,1)} %param.27, bf16[8,1024,4096]{2,1,0:T(8,128)(2,1)} %param.24, f32[4096]{0:T(1024)S(1)} %copy-done.26, f32[8,1024]{1,0:T(8,128)S(1)} %add_rsqrt_fusion), kind=kOutput, calls=%fused_computation.66 | convolution fusion | flops 8724152320 | bytes 72400896 | tf_op jit(solution)/shard_map/bsd,dhe->bshe/dot_general | solution.py:64
  234.7 30.1 %fusion.40 = f32[8,1024,128]{1,2,0:T(8,128)} fusion(bf16[4096,1,128]{2,0,1:T(8,128)(2,1)S(1)} %copy-done.25, bf16[8,1024,4096]{2,1,0:T(8,128)(2,1)} %param.24, f32[4096]{0:T(1024)S(1)} %copy-done.26, f32[8,1024]{1,0:T(8,128)S(1)} %add_rsqrt_fusion), kind=kOutput, calls=%fused_computation.64 | convolution fusion | flops 8724152320 | bytes 72400896 | tf_op jit(solution)/shard_map/bsd,dhe->bshe/dot_general | solution.py:64
  266.6 45.7 %fusion.12 = f32[8,1024,512]{2,1,0:T(8,128)} fusion(bf16[4096,512]{1,0:T(8,128)(2,1)} %param.31, bf16[8,1024,4096]{2,1,0:T(8,128)(2,1)} %param.24, f32[4096]{0:T(1024)S(1)} %copy-done.26, f32[8,1024]{1,0:T(8,128)S(1)} %add_rsqrt_fusion), kind=kOutput, calls=%fused_computation.33 | convolution fusion | flops 34493956096 | bytes 88129536 | tf_op jit(solution)/shard_map/bsd,df->bsf/dot_general | solution.py:70
  313.0 2.6 gather_fusion.12
  315.6 12.0 %fusion.24 = f32[8,1024,512]{2,1,0:T(8,128)} fusion(bf16[8,128,512]{2,1,0:T(8,128)(2,1)S(1)} %gather_fusion.9, bf16[8,1024,128]{1,0,2:T(8,128)(2,1)} %all-gather.15.cloned.1.call-done), kind=kOutput, calls=%fused_computation.47 | convolution fusion | flops 1073741824 | bytes 19922944 | tf_op jit(solution)/shard_map/bsr,brf->bsf/dot_general | solution.py:71
  327.6 11.5 fusion.26
  339.1 52.4 %multiply_convert_fusion = bf16[8,1024,512]{2,1,0:T(8,128)(2,1)} fusion(f32[8,1024,512]{2,1,0:T(8,128)} %fusion.24, f32[8,1024,512]{2,1,0:T(8,128)} %fusion.12, f32[8,1024,512]{2,1,0:T(8,128)} %fusion.26, bf16[4096,512]{1,0:T(8,128)(2,1)} %param.32, bf16[8,1024,4096]{2,1,0:T(8,128)(2,1)} %param.24, f32[4096]{0:T(1024)S(1)} %copy-done.26, ...), kind=kOutput, calls=%fused_computation.25 | convolution fusion | flops 34535899136 | bytes 130072576 | tf_op jit(solution)/shard_map/bsd,df->bsf/dot_general | solution.py:70
  391.6 50.7 %fusion.9 = f32[8,1024,4096]{1,2,0:T(8,128)} fusion(bf16[8,1024,512]{2,1,0:T(8,128)(2,1)} %multiply_convert_fusion, bf16[512,4096]{1,0:T(8,128)(2,1)} %param.33), kind=kOutput, calls=%fused_computation.30 | convolution fusion | flops 34359738368 | bytes 146800640 | tf_op jit(solution)/shard_map/bsf,fd->bsd/dot_general | solution.py:81
  442.3 7.7 add_bitcast_fusion.1
  450.0 5.8 add_bitcast_fusion
  455.9 4.0 fusion.36
  459.9 3.7 convolution_convert_fusion
  463.6 14.1 %fusion.80 = f32[8,1024]{1,0:T(8,128)S(1)} fusion(pred[1024,1024]{0,1:T(8,128)(4,1)} %iota_compare_fusion, bf16[8,1024,64]{1,2,0:T(8,128)(2,1)} %get-tuple-element.11, bf16[8,1024,64]{1,2,0:T(8,128)(2,1)} %get-tuple-element.12, bf16[8,1024,64]{1,2,0:T(8,128)(2,1)S(1)} %get-tuple-element.8, bf16[8,1024,64]{1,2,0:T(8,128)(2,1)S(1)} %get-tuple-element.7), kind=kOutput, calls=%fused_computation.98 | convolution fusion | flops 2189427712 | bytes 5275648 | tf_op jit(solution)/shard_map/sub | solution.py:36
  477.7 6.9 add_convert_fusion.2
  484.6 18.3 %fusion.30 = bf16[8,128,1024]{2,1,0:T(8,128)(2,1)S(1)} fusion(bf16[8,1024,128]{1,2,0:T(8,128)(2,1)} %add_convert_fusion.2, f32[8,1024]{1,0:T(8,128)S(1)} %fusion.80, pred[1024,1024]{0,1:T(8,128)(4,1)} %iota_compare_fusion, bf16[8,1024,64]{1,2,0:T(8,128)(2,1)} %get-tuple-element.11, bf16[8,1024,64]{1,2,0:T(8,128)(2,1)} %get-tuple-element.12, ...), kind=kOutput, calls=%fused_computation.57 | convolution fusion | flops 4346356736 | bytes 9469952 | tf_op jit(solution)/shard_map/bhqk,bkhd->bqhd/dot_general | solution.py:37
  503.0 2.2 fusion.33
  505.4 67.0 %add_convert_fusion = bf16[8,1024,4096]{1,2,0:T(8,128)(2,1)} fusion(f32[8,1024,4096]{1,2,0:T(8,128)} %fusion.9, bf16[8,128,1024]{2,1,0:T(8,128)(2,1)S(1)} %fusion.30, bf16[1,128,4096]{2,1,0:T(8,128)(2,1)S(1)} %copy-done), kind=kOutput, calls=%fused_computation.20 | convolution fusion | flops 8657043456 | bytes 204472320 | tf_op jit(solution)/shard_map/bshe,hed->bsd/dot_general | solution.py:81
  573.9 3.1 constant_dynamic-slice_fusion
  577.0 3.1 copy.77
  581.6 29.0 %all-reduce.3.cloned.1.call-done = (bf16[8,1024,128]{2,1,0:T(8,128)(2,1)}, bf16[8,1024,128]{2,1,0:T(8,128)(2,1)}) async-done(((bf16[8,1024,128]{2,1,0:T(8,128)(2,1)}, bf16[8,1024,128]{2,1,0:T(8,128)(2,1)}), (bf16[8,1024,128]{2,1,0:T(8,128)(2,1)}, bf16[8,1024,128]{2,1,0:T(8,128)(2,1)})) %all-reduce.3.cloned.1.call-update) | async-done | bytes 4194320 | tf_op jit(solution)/shard_map/psum | solution.py:79
  610.6 4.3 fusion.81
  614.9 283.4 %reduce-scatter.2.cloned.1.call-done = bf16[8,1024,128]{1,2,0:T(8,128)(2,1)} async-done(((bf16[8,1024,4096]{1,2,0:T(8,128)(2,1)}), bf16[8,1024,128]{1,2,0:T(8,128)(2,1)}) %reduce-scatter.2.cloned.1.call-update) | async-done | bytes 2097168 | tf_op jit(solution)/shard_map/reduce_scatter | solution.py:82
  898.3 6.0 add_convert_fusion.1
  904.4 196.3 %all-gather.17.cloned.1.call-done = bf16[8,1024,4096]{1,2,0:T(8,128)(2,1)} async-done(((bf16[8,1024,128]{1,2,0:T(8,128)(2,1)}), bf16[8,1024,4096]{1,2,0:T(8,128)(2,1)}) %all-gather.17.cloned.1.call-update) | async-done | bytes 67108880 | tf_op jit(solution)/shard_map/all_gather | solution.py:87
  1100.7 78.8 %copy.56 = bf16[8,1024,4096]{2,1,0:T(8,128)(2,1)} copy(bf16[8,1024,4096]{1,2,0:T(8,128)(2,1)} %all-gather.17.cloned.1.call-done) | data formatting | bytes 134217728 | tf_op jit(solution)/shard_map/all_gather | solution.py:87
  (104 shorter events, 21.9 us)
Async XLA Ops:
  6.5 498.8 %copy-start = (bf16[1,128,4096]{2,1,0:T(8,128)(2,1)S(1)}, bf16[1,128,4096]{2,1,0:T(8,128)(2,1)}, u32[]{:S(2)}) copy-start(bf16[1,128,4096]{2,1,0:T(8,128)(2,1)} %param.30) | copy-start | bytes 3145732
  6.6 309.1 %all-gather.15.cloned.1.call-start = ((), (), s32[]{:S(2)}) async-start(), calls=%async_computation.5 | async-start | bytes 2162688 | tf_op jit(solution)/shard_map/all_gather | solution.py:60
  7.3 305.7 %copy-start.23 = (s32[1024]{0:T(1024)}, s32[1024]{0:T(1024)S(1)}, u32[]{:S(2)}) copy-start(s32[1024]{0:T(1024)S(1)} %pad_clamp_fusion) | copy-start | bytes 12292
  7.3 21.0 %copy-start.1 = (bf16[2,4096,4]{1,2,0:T(4,128)(2,1)S(1)}, bf16[2,4096,4]{1,2,0:T(4,128)(2,1)}, u32[]{:S(2)}) copy-start(bf16[2,4096,4]{1,2,0:T(4,128)(2,1)} %param.44) | copy-start | bytes 196612
  29.1 26.5 %copy-start.2 = (bf16[2,4096,4]{1,2,0:T(4,128)(2,1)S(1)}, bf16[2,4096,4]{1,2,0:T(4,128)(2,1)}, u32[]{:S(2)}) copy-start(bf16[2,4096,4]{1,2,0:T(4,128)(2,1)} %param.42) | copy-start | bytes 196612
  55.6 272.0 %all-gather.13.cloned.1.call-start = ((), (), s32[]{:S(2)}) async-start(), calls=%async_computation.4 | async-start | bytes 2162688 | tf_op jit(solution)/shard_map/all_gather | solution.py:60
  56.4 26.5 %copy-start.3 = (bf16[2,4096,4]{1,2,0:T(4,128)(2,1)S(1)}, bf16[2,4096,4]{1,2,0:T(4,128)(2,1)}, u32[]{:S(2)}) copy-start(bf16[2,4096,4]{1,2,0:T(4,128)(2,1)} %param.34) | copy-start | bytes 196612
  82.9 359.4 %all-gather.9.cloned.1.call-start = ((), (), s32[]{:S(2)}) async-start(), calls=%async_computation.2 | async-start | bytes 2162688 | tf_op jit(solution)/shard_map/all_gather | solution.py:60
  83.7 27.1 %copy-start.4 = (bf16[2,4096,4]{1,2,0:T(4,128)(2,1)S(1)}, bf16[2,4096,4]{1,2,0:T(4,128)(2,1)}, u32[]{:S(2)}) copy-start(bf16[2,4096,4]{1,2,0:T(4,128)(2,1)} %param.36) | copy-start | bytes 196612
  110.2 339.8 %all-gather.11.cloned.1.call-start = ((), (), s32[]{:S(2)}) async-start(), calls=%async_computation.3 | async-start | bytes 2162688 | tf_op jit(solution)/shard_map/all_gather | solution.py:60
  111.6 26.5 %copy-start.5 = (bf16[2,4096,4]{1,2,0:T(4,128)(2,1)S(1)}, bf16[2,4096,4]{1,2,0:T(4,128)(2,1)}, u32[]{:S(2)}) copy-start(bf16[2,4096,4]{1,2,0:T(4,128)(2,1)} %param.38) | copy-start | bytes 196612
  138.0 339.7 %all-gather.7.cloned.1.call-start = ((), (), s32[]{:S(2)}) async-start(), calls=%async_computation.1 | async-start | bytes 2162688 | tf_op jit(solution)/shard_map/all_gather | solution.py:60
  138.9 28.1 %copy-start.15 = (bf16[2,1,128,128]{3,2,1,0:T(8,128)(2,1)S(1)}, bf16[2,1,128,128]{3,2,1,0:T(8,128)(2,1)}, u32[]{:S(2)}) copy-start(bf16[2,1,128,128]{3,2,1,0:T(8,128)(2,1)} %param.40) | copy-start | bytes 196612
  138.9 29.3 %copy-start.24 = (bf16[4096,1,128]{2,0,1:T(8,128)(2,1)S(1)}, bf16[4096,1,128]{2,0,1:T(8,128)(2,1)}, u32[]{:S(2)}) copy-start(bf16[4096,1,128]{2,0,1:T(8,128)(2,1)} %param.29) | copy-start | bytes 3145732
  165.4 445.2 %all-reduce.3.cloned.1.call-start = ((), (), s32[]{:S(2)}) async-start(), calls=%async_computation.8 | async-start | bytes 8388608 | tf_op jit(solution)/shard_map/psum | solution.py:79
  168.3 30.0 %copy-start.16 = (bf16[2,128,1,128]{3,1,2,0:T(8,128)(2,1)S(1)}, bf16[2,128,1,128]{3,1,2,0:T(8,128)(2,1)}, u32[]{:S(2)}) copy-start(bf16[2,128,1,128]{3,1,2,0:T(8,128)(2,1)} %param.39) | copy-start | bytes 196612
  199.6 32.0 %copy-start.17 = (bf16[2,128,1,128]{3,1,2,0:T(8,128)(2,1)S(1)}, bf16[2,128,1,128]{3,1,2,0:T(8,128)(2,1)}, u32[]{:S(2)}) copy-start(bf16[2,128,1,128]{3,1,2,0:T(8,128)(2,1)} %param.35) | copy-start | bytes 196612
  199.6 35.1 %copy-start.25 = (bf16[4096,1,128]{2,0,1:T(8,128)(2,1)S(1)}, bf16[4096,1,128]{2,0,1:T(8,128)(2,1)}, u32[]{:S(2)}) copy-start(bf16[4096,1,128]{2,0,1:T(8,128)(2,1)} %param.28) | copy-start | bytes 3145732
  234.6 30.1 %copy-start.18 = (bf16[2,128,1,128]{3,1,2,0:T(8,128)(2,1)S(1)}, bf16[2,128,1,128]{3,1,2,0:T(8,128)(2,1)}, u32[]{:S(2)}) copy-start(bf16[2,128,1,128]{3,1,2,0:T(8,128)(2,1)} %param.37) | copy-start | bytes 196612
  234.6 31.3 %copy-start.7 = (bf16[2,128,512]{2,1,0:T(8,128)(2,1)S(1)}, bf16[2,128,512]{2,1,0:T(8,128)(2,1)}, u32[]{:S(2)}) copy-start(bf16[2,128,512]{2,1,0:T(8,128)(2,1)} %param.45) | copy-start | bytes 786436
  266.6 45.7 %copy-start.8 = (bf16[2,128,512]{2,1,0:T(8,128)(2,1)S(1)}, bf16[2,128,512]{2,1,0:T(8,128)(2,1)}, u32[]{:S(2)}) copy-start(bf16[2,128,512]{2,1,0:T(8,128)(2,1)} %param.43) | copy-start | bytes 786436
  391.6 50.8 %copy-start.22 = (bf16[8,128,128]{2,1,0:T(8,128)(2,1)S(1)}, bf16[8,128,128]{2,1,0:T(8,128)(2,1)}, u32[]{:S(2)}) copy-start(bf16[8,128,128]{2,1,0:T(8,128)(2,1)} %gather_fusion.3) | copy-start | bytes 786436
  442.3 7.8 copy-start.21
  442.3 13.6 %copy-start.13 = (f32[1024,64]{0,1:T(8,128)S(1)}, f32[1024,64]{0,1:T(8,128)}, u32[]{:S(2)}) copy-start(f32[1024,64]{0,1:T(8,128)} %get-tuple-element.13) | copy-start | bytes 786436
  450.0 9.8 slice-start
  459.8 17.8 %copy-start.9 = (bf16[8,1024,64]{1,2,0:T(8,128)(2,1)}, bf16[8,1024,64]{1,2,0:T(8,128)(2,1)S(1)}, u32[]{:S(2)}) copy-start(bf16[8,1024,64]{1,2,0:T(8,128)(2,1)S(1)} %get-tuple-element.7) | copy-start | bytes 3145732
  459.9 17.8 %copy-start.10 = (bf16[8,1024,64]{1,2,0:T(8,128)(2,1)}, bf16[8,1024,64]{1,2,0:T(8,128)(2,1)S(1)}, u32[]{:S(2)}) copy-start(bf16[8,1024,64]{1,2,0:T(8,128)(2,1)S(1)} %get-tuple-element.8) | copy-start | bytes 3145732
  463.6 14.1 %copy-start.12 = (bf16[8,128,128]{2,1,0:T(8,128)(2,1)S(1)}, bf16[8,128,128]{2,1,0:T(8,128)(2,1)}, u32[]{:S(2)}) copy-start(bf16[8,128,128]{2,1,0:T(8,128)(2,1)} %gather_fusion.1) | copy-start | bytes 786436
  484.6 18.3 %copy-start.11 = (bf16[8,128,128]{2,1,0:T(8,128)(2,1)S(1)}, bf16[8,128,128]{2,1,0:T(8,128)(2,1)}, u32[]{:S(2)}) copy-start(bf16[8,128,128]{2,1,0:T(8,128)(2,1)} %gather_fusion.10) | copy-start | bytes 786436
  505.3 393.0 %reduce-scatter.2.cloned.1.call-start = ((), (), s32[]{:S(2)}) async-start(), calls=%async_computation.6 | async-start | bytes 69206016 | tf_op jit(solution)/shard_map/reduce_scatter | solution.py:82
  572.4 7.7 copy-start.20
  572.4 528.2 %all-gather.17.cloned.1.call-start = ((), (), s32[]{:S(2)}) async-start(), calls=%async_computation.7 | async-start | bytes 69206016 | tf_op jit(solution)/shard_map/all_gather | solution.py:87
  (5 other events, 15.4 us)
Sparse Core Ops, SparseCore 0:
  55.7 42.7 all-gather.14
  100.5 37.5 all-gather.12
  140.3 37.4 all-gather.8
  179.7 37.4 all-gather.10
  219.2 37.5 all-gather.6
  505.4 105.1 all-reduce.2
  614.4 283.8 reduce-scatter.1
  904.5 196.1 all-gather.16
where the time goes:
time: 1200 us; the launch traced here: 1190 us
  matrix products  529 us (44%)
  waiting for transfers between devices  509 us (42%)
  local copies, waits for them, and re-layouts  104 us (9%)
  other arithmetic  28.8 us (2%)
  between operations  14.5 us (1%)
    reduce_scatter x1, waiting for transfers between devices, local_layer(): lax.psum_scatter(base_part, 'tensor', scatter_dimension=2, tiled=True)  283 us
    all_gather x1, waiting for transfers between devices, local_layer(): return lax.all_gather(y_share, 'tensor', axis=2, tiled=True)  196 us
    dot_general x5, matrix products, gather_mid(): jnp.einsum('bsd,bdr->bsr', normed, a_stack[adapter_ids], preferred_elemen...  129 us
    dot_general x2, matrix products, ffn_proj(): jnp.einsum('bsd,df->bsf', normed, weight, preferred_element_type=jnp.floa...  98.1 us
    dot_general x3, matrix products, head_proj(): jnp.einsum('bsd,dhe->bshe', normed, weight, preferred_element_type=jnp.fl...  92.1 us
    all_gather x1, local copies, waits for them, and re-layouts, local_layer(): return lax.all_gather(y_share, 'tensor', axis=2, tiled=True)  78.8 us
    dot_general x1, matrix products, local_layer(): jnp.einsum('bshe,hed->bsd', attended, w_out, preferred_element_type=jnp.f...  67 us
    dot_general x1, matrix products, local_layer(): jnp.einsum('bsf,fd->bsd', mlp_mixed, w_down, preferred_element_type=jnp.f...  50.7 us
  transfers between devices with their start and end apart: 8, of which 3 were waited for; matrix products, arithmetic and copies ran while one was open for 42% of the time, Pallas kernels for 0%

commit v1 on v0

v1 whole, which is shorter than its diff:
```python
import functools
import math

import jax
import jax.numpy as jnp
from jax import lax
from jax.experimental import pallas as pl
from jax.experimental.pallas import tpu as pltpu
from jax.sharding import PartitionSpec as P

ALPHA = 16
EPS = 1e-5
ROPE_BASE = 10000.0
MESH = pl.DeviceIdType.MESH
BF = jnp.bfloat16

def rms_norm(x_blk, norm_gain):
    x_f32 = x_blk.astype(jnp.float32)
    return (x_f32 * lax.rsqrt(jnp.mean(x_f32 * x_f32, axis=-1, keepdims=True) + EPS) * norm_gain).astype(jnp.bfloat16)


def rope_tables(seq_len, head_dim):
    half_dim = head_dim // 2
    inv_freq = ROPE_BASE ** (-jnp.arange(half_dim, dtype=jnp.float32) / half_dim)
    angles = jnp.arange(seq_len, dtype=jnp.float32)[:, None] * inv_freq[None, :]
    return jnp.cos(angles)[:, None, :], jnp.sin(angles)[:, None, :]


def rope_rotate(vals, cos_t, sin_t):
    half_dim = vals.shape[-1] // 2
    first = vals[..., :half_dim]
    second = vals[..., half_dim:]
    return jnp.concatenate([first * cos_t - second * sin_t, second * cos_t + first * sin_t], axis=-1)


def causal_attention(query_rot, key_rot, value_heads):
    seq_len = query_rot.shape[1]
    head_dim = query_rot.shape[3]
    scores = jnp.einsum('bqhd,bkhd->bhqk', query_rot, key_rot, preferred_element_type=jnp.float32) / math.sqrt(head_dim)
    causal = jnp.arange(seq_len)[:, None] >= jnp.arange(seq_len)[None, :]
    probs_bf = jax.nn.softmax(jnp.where(causal, scores, -1e30), axis=-1).astype(jnp.bfloat16)
    return jnp.einsum('bhqk,bkhd->bqhd', probs_bf, value_heads, preferred_element_type=jnp.float32).astype(jnp.bfloat16)


def comm_kernel(cfg, ids_ref, part_ref, midp_ref, x_ref, bod_ref, stage_ref,
                psend, pown, l0, r0, l1f, l1d, l1s, s1, r1, l2f, l2d, l2s, s2, r2, xrow, yrow, bodv,
                ld_sem, d2d_s, d2d_r, p1_s, p1_r, p2_s, p2_r, aga_s, aga_r, agb_s, agb_r, dd_s, dd_r, loc_sem):
    (N, R, NT, TT, W, D, scale, tiles_per_seq) = cfg
    HALF = TT // 2; B1 = HALF // R; B2 = B1 // R; WH = W // 2; DH = D // 2
    idx = lax.axis_index("tensor")
    c = lax.rem(idx, 2)
    xx = lax.rem(idx // 2, R)
    yy = idx // (2 * R)
    q1 = jnp.where(c == 0, xx, yy); q2 = jnp.where(c == 0, yy, xx)
    st1 = 2 + (2 * R - 2) * c; st2 = 2 * R - (2 * R - 2) * c
    b1 = idx - q1 * st1; b2 = idx - q2 * st2
    def nb(base, st, q, d): return base + lax.rem(q + d + R, R) * st
    plus1, minus1 = nb(b1, st1, q1, 1), nb(b1, st1, q1, -1)
    plus2, minus2 = nb(b2, st2, q2, 1), nb(b2, st2, q2, -1)
    mate = idx + 1 - 2 * c
    peers = (mate, plus1, minus1, plus2, minus2)

    bar = pltpu.get_barrier_semaphore()
    for p in peers:
        pl.semaphore_signal(bar, inc=1, device_id={"tensor": p}, device_id_type=MESH)
    pl.semaphore_wait(bar, len(peers))

    def rc(src, dst, ss, rs, dev):
        return pltpu.make_async_remote_copy(src_ref=src, dst_ref=dst, send_sem=ss, recv_sem=rs, device_id={"tensor": dev}, device_id_type=MESH)

    bcp = pltpu.make_async_copy(bod_ref, bodv, loc_sem.at[0])
    bcp.start(); bcp.wait()

    def blk(q, d, rows): return pl.ds(pl.multiple_of(lax.rem(q + d + R, R) * rows, rows), rows)
    A, B = pl.ds(0, WH), pl.ds(WH, WH)
    DA, DB = pl.ds(0, DH), pl.ds(DH, DH)

    def loads(t, half, buf, k):
        rows = pl.ds(pl.multiple_of(t * TT + half * HALF, HALF), HALF)
        return (pltpu.make_async_copy(part_ref.at[rows, :], buf.at[:, pl.ds(0, D)], ld_sem.at[k, 0]),
                pltpu.make_async_copy(midp_ref.at[rows, :], buf.at[:, pl.ds(D, W - D)], ld_sem.at[k, 1]))

    def d2d(t):
        s = lax.rem(t, 2)
        return rc(psend, l0.at[s], d2d_s, d2d_r.at[s], mate)
    def s1_copies(src, q, rows, lf, ld, ss, rs, plus, minus):
        return (rc(src.at[blk(q, 2, rows), A], lf.at[0], ss.at[0], rs.at[0], plus),
                rc(src.at[blk(q, 2, rows), B], lf.at[1], ss.at[1], rs.at[1], minus),
                rc(src.at[blk(q, 1, rows), B], ld.at[0], ss.at[2], rs.at[2], plus),
                rc(src.at[blk(q, -1, rows), A], ld.at[1], ss.at[3], rs.at[3], minus))
    def s2_copies(sm, ls, ss, rs, plus, minus):
        return (rc(sm.at[0], ls.at[0], ss.at[4], rs.at[4], plus),
                rc(sm.at[1], ls.at[1], ss.at[5], rs.at[5], minus))
    def p1s1(t): return s1_copies(r0, q1, B1, l1f, l1d, p1_s, p1_r, plus1, minus1)
    def p1s2(t): return s2_copies(s1, l1s, p1_s, p1_r, plus1, minus1)
    def p2s1(t):
        s = lax.rem(t, 2)
        return s1_copies(r1.at[s], q2, B2, l2f.at[s], l2d.at[s], p2_s.at[s], p2_r.at[s], plus2, minus2)
    def p2s2(t):
        s = lax.rem(t, 2)
        return s2_copies(s2, l2s.at[s], p2_s.at[s], p2_r.at[s], plus2, minus2)
    def row0(t): return t * TT + c * HALF
    def rows_a(t, d): return pl.ds(pl.multiple_of(row0(t) + q1 * B1 + lax.rem(q2 + d + R, R) * B2, B2), B2)
    def rows_b(t, d): return pl.ds(pl.multiple_of(row0(t) + lax.rem(q1 + d + R, R) * B1, B1), B1)
    def sl(t): return lax.rem(t, 4)
    def aga1(t):
        s = sl(t); r = rows_a(t, 0)
        return (rc(yrow, stage_ref.at[r, :], aga_s.at[s, 0], aga_r.at[s, 0], plus2),
                rc(yrow, stage_ref.at[r, :], aga_s.at[s, 1], aga_r.at[s, 1], minus2))
    def aga2(t):
        s = sl(t)
        return (rc(stage_ref.at[rows_a(t, -1), DA], stage_ref.at[rows_a(t, -1), DA], aga_s.at[s, 2], aga_r.at[s, 2], plus2),
                rc(stage_ref.at[rows_a(t, 1), DB], stage_ref.at[rows_a(t, 1), DB], aga_s.at[s, 3], aga_r.at[s, 3], minus2))
    def agb1(t):
        s = sl(t); r = rows_b(t, 0)
        return (rc(stage_ref.at[r, :], stage_ref.at[r, :], agb_s.at[s, 0], agb_r.at[s, 0], plus1),
                rc(stage_ref.at[r, :], stage_ref.at[r, :], agb_s.at[s, 1], agb_r.at[s, 1], minus1))
    def agb2(t):
        s = sl(t)
        return (rc(stage_ref.at[rows_b(t, -1), DA], stage_ref.at[rows_b(t, -1), DA], agb_s.at[s, 2], agb_r.at[s, 2], plus1),
                rc(stage_ref.at[rows_b(t, 1), DB], stage_ref.at[rows_b(t, 1), DB], agb_s.at[s, 3], agb_r.at[s, 3], minus1))
    def dd(t):
        s = sl(t); r = pl.ds(pl.multiple_of(row0(t), HALF), HALF)
        return rc(stage_ref.at[r, :], stage_ref.at[r, :], dd_s.at[s], dd_r.at[s], mate)
    def yloc(t): return pltpu.make_async_copy(yrow, stage_ref.at[rows_a(t, 0), :], loc_sem.at[1])
    def xload(t): return pltpu.make_async_copy(x_ref.at[rows_a(t, 0), :], xrow, loc_sem.at[2])

    def start(cs):
        for cp in cs: cp.start()
    def wrecv(cs):
        for cp in cs: cp.wait_recv()
    def wsend(cs):
        for cp in cs: cp.wait_send()

    def comb(src, q, rows, lf, ld, sm, dst):
        sm[0] = src[blk(q, 1, rows), A] + lf[0]
        sm[1] = src[blk(q, -1, rows), B] + lf[1]
        dst[:, A] = src[blk(q, 0, rows), A] + ld[1]
        dst[:, B] = src[blk(q, 0, rows), B] + ld[0]

    def e1(t):
        wrecv(p1s1(t)); wsend(p1s1(t))
        @pl.when(t >= 1)
        def _():
            wsend(p1s2(t - 1))
        comb(r0, q1, B1, l1f, l1d, s1, r1.at[lax.rem(t, 2)])
        start(p1s2(t))
    def e2(t):
        wrecv(p1s2(t))
        s = lax.rem(t, 2)
        r1[s, :, A] = r1[s, :, A] + l1s[0]
        r1[s, :, B] = r1[s, :, B] + l1s[1]
        start(p2s1(t))
    def e3(t):
        s = lax.rem(t, 2)
        wrecv(p2s1(t)); wsend(p2s1(t))
        @pl.when(t >= 1)
        def _(): wsend(p2s2(t - 1))
        comb(r1.at[s], q2, B2, l2f.at[s], l2d.at[s], s2, r2)
        start(p2s2(t))
        xload(t).start()
    def e4(t):
        s = lax.rem(t, 2)
        wrecv(p2s2(t))
        xload(t).wait()
        i = ids_ref[t // tiles_per_seq]
        r2[:, A] = r2[:, A] + l2s[s, 0]
        r2[:, B] = r2[:, B] + l2s[s, 1]
        mid = r2[:, pl.ds(D, W - D)]
        lor = jnp.dot(mid, bodv[i], preferred_element_type=jnp.float32)
        y = xrow[...].astype(jnp.float32) + r2[:, pl.ds(0, D)].astype(jnp.float32) + scale * lor
        yrow[...] = y.astype(BF)
        yloc(t).start()
        start(aga1(t))
    def e5(t):
        yloc(t).wait(); wsend(aga1(t)); wrecv(aga1(t)); start(aga2(t))
    def e6(t):
        wrecv(aga2(t)); start(agb1(t))
    def e7(t):
        wrecv(agb1(t)); start(agb2(t))
    def e8(t):
        wrecv(agb2(t)); start((dd(t),))
    def e9(t):
        wrecv((dd(t),)); wsend((dd(t),)); wsend(agb2(t)); wsend(agb1(t)); wsend(aga2(t))

    LAST = NT - 1
    def guard(t, f):
        @pl.when(jnp.logical_and(t >= 0, t < NT))
        def _(): f(t)

    for cp in loads(0, 1 - c, psend, 0) + loads(0, c, pown, 1): cp.start()

    def produce(t):
        for cp in loads(t, 1 - c, psend, 0): cp.wait()
        d2d(t).start()
        for cp in loads(t, c, pown, 1): cp.wait()
        d2d(t).wait_recv()
        r0[...] = pown[...] + l0[lax.rem(t, 2)]
        start(p1s1(t))
        d2d(t).wait_send()
        @pl.when(t + 1 < NT)
        def _():
            for cp in loads(t + 1, 1 - c, psend, 0) + loads(t + 1, c, pown, 1): cp.start()

    def body(it, _):
        guard(it - 1, e1)
        guard(it - 4, e7)
        guard(it - 2, e3)
        guard(it - 3, e5)
        guard(it - 1, e2)
        guard(it - 4, e8)
        guard(it - 2, e4)
        guard(it - 3, e6)
        guard(it - 5, e9)
        guard(it, produce)
        return 0
    lax.fori_loop(0, NT + 6, body, 0)
    wsend(p1s2(LAST)); wsend(p2s2(LAST));

def comm(mesh, part, midp, x, bod, ids, scale, tiles_per_seq, TT=512):
    N = mesh.shape["tensor"]; R = math.isqrt(N // 2)
    T, D = part.shape; W = D + midp.shape[1]
    NT = T // TT; HALF = TT // 2; B1 = HALF // R; B2 = B1 // R; WH = W // 2
    cfg = (N, R, NT, TT, W, D, scale, tiles_per_seq)
    V = pltpu.VMEM; S = pltpu.SemaphoreType.DMA
    return pl.pallas_call(
        functools.partial(comm_kernel, cfg), name="rsag",
        out_shape=jax.ShapeDtypeStruct((T, D), BF),
        in_specs=[pl.BlockSpec(memory_space=pltpu.SMEM)] + [pl.BlockSpec(memory_space=pl.ANY)] * 4,
        out_specs=pl.BlockSpec(memory_space=pl.ANY),
        scratch_shapes=[V((HALF, W), BF), V((HALF, W), BF), V((2, HALF, W), BF), V((HALF, W), BF),
                        V((2, B1, WH), BF), V((2, B1, WH), BF), V((2, B1, WH), BF), V((2, B1, WH), BF), V((2, B1, W), BF),
                        V((2, 2, B2, WH), BF), V((2, 2, B2, WH), BF), V((2, 2, B2, WH), BF), V((2, B2, WH), BF), V((B2, W), BF),
                        V((B2, D), BF), V((B2, D), BF), V(bod.shape, BF),
                        S((2, 2)), S, S((2,)), S((6,)), S((6,)), S((2, 6)), S((2, 6)), S((4, 4)), S((4, 4)), S((4, 4)), S((4, 4)), S((4,)), S((4,)), S((3,))],
        compiler_params=pltpu.CompilerParams(collective_id=0, has_side_effects=True, vmem_limit_bytes=60 * 2**20),
    )(ids, part, midp, x, bod)


def solution(mesh):
    batch_spec = P('data', None, None)
    head_cols = P(None, 'tensor', None)
    head_rows = P('tensor', None, None)
    ff_cols = P(None, 'tensor')
    ff_rows = P('tensor', None)
    last_split = P(None, None, 'tensor')
    b_heads = P(None, None, 'tensor', None)
    a_heads = P(None, 'tensor', None, None)
    in_specs = (batch_spec, P('data'), P(None), head_cols, head_cols, head_cols, head_rows, ff_cols, ff_cols, ff_rows, last_split, b_heads, last_split, b_heads, last_split, b_heads, a_heads, last_split, last_split, last_split, last_split, last_split, head_cols, last_split)

    def local_layer(x_blk, adapter_ids, norm_gain, w_query, w_key, w_value, w_out, w_gate, w_up, w_down, a_query, b_query, a_key, b_key, a_value, b_value, a_out, b_out, a_gate, b_gate, a_up, b_up, a_down, b_down):
        seq_len = x_blk.shape[1]
        rank = a_out.shape[-1]
        scale = ALPHA / rank
        normed = rms_norm(x_blk, norm_gain)
        cos_t, sin_t = rope_tables(seq_len, w_query.shape[-1])
        n_dev = mesh.shape['tensor']
        stacks = jnp.stack([a_query, a_key, a_value, a_gate, a_up])
        gathered = lax.all_gather(jnp.transpose(stacks, (1, 0, 3, 2)).reshape(-1, stacks.shape[2]), 'tensor', axis=0, tiled=True)
        gathered = gathered.reshape(n_dev, stacks.shape[1], stacks.shape[0], rank // n_dev, stacks.shape[2])
        a_all = jnp.transpose(gathered, (1, 2, 0, 3, 4)).reshape(stacks.shape[1], stacks.shape[0] * rank, stacks.shape[2])
        mids = jnp.einsum('bsd,brd->bsr', normed, a_all[adapter_ids], preferred_element_type=jnp.float32).astype(jnp.bfloat16)
        head = w_query.shape[-1]
        width = w_query.shape[1] * head
        w_in = jnp.concatenate([w.reshape(w.shape[0], -1) for w in (w_query, w_key, w_value, w_gate, w_up)], axis=1)

        def lora(k, b_stack):
            flat = b_stack.reshape(b_stack.shape[0], rank, -1)
            return scale * jnp.einsum('bsr,bre->bse', mids[:, :, k * rank:(k + 1) * rank], flat[adapter_ids], preferred_element_type=jnp.float32)

        base = jnp.einsum('bsd,de->bse', normed, w_in, preferred_element_type=jnp.float32)
        ff = w_gate.shape[1]
        heads = lambda k, b: (base[:, :, k * width:(k + 1) * width] + lora(k, b)).reshape(*x_blk.shape[:2], -1, head)
        query_rot = rope_rotate(heads(0, b_query), cos_t, sin_t).astype(jnp.bfloat16)
        key_rot = rope_rotate(heads(1, b_key), cos_t, sin_t).astype(jnp.bfloat16)
        value_heads = heads(2, b_value).astype(jnp.bfloat16)
        gate = base[:, :, 3 * width:3 * width + ff] + lora(3, b_gate)
        up = base[:, :, 3 * width + ff:] + lora(4, b_up)
        attended = causal_attention(query_rot, key_rot, value_heads)
        mlp_mixed = (jax.nn.silu(gate) * up).astype(jnp.bfloat16)
        mid_out = jnp.einsum('bshe,bher->bsr', attended, a_out[adapter_ids], preferred_element_type=jnp.float32)
        mid_down = jnp.einsum('bsf,bfr->bsr', mlp_mixed, a_down[adapter_ids], preferred_element_type=jnp.float32)
        mid_part = jnp.concatenate([mid_out, mid_down], axis=-1).astype(jnp.bfloat16)
        base_part = (jnp.einsum('bshe,hed->bsd', attended, w_out, preferred_element_type=jnp.float32) + jnp.einsum('bsf,fd->bsd', mlp_mixed, w_down, preferred_element_type=jnp.float32)).astype(jnp.bfloat16)
        b_both = lax.all_gather(jnp.concatenate([b_out, b_down], axis=1), 'tensor', axis=0)
        b_both = jnp.moveaxis(b_both, 0, 2).reshape(b_both.shape[1], b_both.shape[2], -1)
        seqs, _, width_out = x_blk.shape
        tile = seq_len // 2
        out = comm(mesh, base_part.reshape(-1, width_out), mid_part.reshape(-1, mid_part.shape[-1]), x_blk.reshape(-1, width_out), b_both, adapter_ids, scale, 2, tile)
        return out.reshape(x_blk.shape)

    return jax.shard_map(local_layer, mesh=mesh, in_specs=in_specs, out_specs=batch_spec, check_vma=False)
```

time: 1200 us -> 1110 us (0.925)
  waiting for transfers between devices: 509 us -> 0.13 us
  Pallas kernels: 0 us -> 486 us
  matrix products: 529 us -> 381 us
  local copies, waits for them, and re-layouts: 104 us -> 176 us
    pallas_call x0 -> x1, Pallas kernels: none -> 486 us  [comm(): pl.pallas_call(functools.partial(comm_kernel, cfg), name='rsag', out_shap...]
    reduce_scatter x1 -> x0, waiting for transfers between devices: 283 us -> none  [local_layer(): lax.psum_scatter(base_part, 'tensor', scatter_dimension=2, tiled=True)]
    all_gather x6 -> x2, waiting for transfers between devices: 196 us -> 0.02 us  [the longest x1 0.02 us: local_layer(): lax.all_gather(jnp.concatenate([b_out, b_down], axis=1), 'tensor', axis=0)]
    dot_general x17 -> x7, matrix products: 373 us -> 220 us  [the longest x1 115 us: local_layer(): jnp.einsum('bsd,de->bse', normed, w_in, preferred_element_type=jnp.float32)]
    all_gather x1, local copies, waits for them, and re-layouts: 78.8 us -> 6.84 us  [local_layer(): lax.all_gather(jnp.concatenate([b_out, b_down], axis=1), 'tensor', axis=0)]
    unnamed x59 -> x58, local copies, waits for them, and re-layouts: 3.95 us -> 71.7 us
    reshape x0 -> x4, local copies, waits for them, and re-layouts: none -> 43.3 us  [the longest x2 35.2 us: local_layer(): gathered.reshape(n_dev, stacks.shape[1], stacks.shape[0], rank // n_dev,...]
    gather x12 -> x10, local copies, waits for them, and re-layouts: 11 us -> 47.5 us  [the longest x5 40.4 us: local_layer(): a_all[adapter_ids]]
  transfers between devices with their start and end apart: 8 -> 2, of which waited for: 3 -> 0; matrix products, arithmetic and copies ran while one was open for 42% -> 17% of each run, Pallas kernels for 0% -> 0%
where the time goes in v1:
time: 1110 us; the launch traced here: 1100 us
  Pallas kernels  486 us (44%)
  matrix products  381 us (34%)
  local copies, waits for them, and re-layouts  176 us (16%)
  other arithmetic  39.4 us (4%)
  between operations  14 us (1%)
    pallas_call x1, Pallas kernels, comm(): pl.pallas_call(functools.partial(comm_kernel, cfg), name='rsag', out_shap...  486 us
    dot_general x1, matrix products, local_layer(): jnp.einsum('bsd,de->bse', normed, w_in, preferred_element_type=jnp.float32)  115 us
    unnamed x58, local copies, waits for them, and re-layouts  71.7 us
    dot_general x1, matrix products, local_layer(): jnp.einsum('bshe,hed->bsd', attended, w_out, preferred_element_type=jnp.f...  65.2 us
    dot_general x1, matrix products, local_layer(): jnp.einsum('bsd,brd->bsr', normed, a_all[adapter_ids], preferred_element_...  59.9 us
    dot_general x1, matrix products, local_layer(): jnp.einsum('bsf,fd->bsd', mlp_mixed, w_down, preferred_element_type=jnp.f...  52 us
    dot_general x5, matrix products, lora(): jnp.einsum('bsr,bre->bse', mids[:, :, k * rank:(k + 1) * rank], flat[adap...  45.1 us
    gather x5, local copies, waits for them, and re-layouts, local_layer(): a_all[adapter_ids]  40.4 us
  transfers between devices with their start and end apart: 2, of which 0 were waited for; matrix products, arithmetic and copies ran while one was open for 17% of the time, Pallas kernels for 0%

profile of v1, /device:TPU:97, one launch (start us, length us, event | category | flops | bytes accessed | tf_op | source)
XLA Modules:
  0.0 1096.7 jit_solution(5611732223057198020)
XLA Ops:
  15.8 21.0 %fusion.1 = f32[8,1024]{1,0:T(8,128)S(1)} fusion(bf16[8,1024,4096]{2,1,0:T(8,128)(2,1)} %param.24), kind=kLoop, calls=%fused_computation.13 | loop fusion | flops 100655104 | bytes 67141632 | tf_op jit(solution)/shard_map/reduce_sum | solution.py:19
  40.6 2.9 fusion.58
  52.3 2.3 bitcast_dynamic-update-slice_fusion
  54.6 4.7 constant_dynamic-update-slice_fusion.1
  59.3 2.3 constant_dynamic-update-slice_fusion
  61.7 114.9 %fusion.6 = f32[8,1024,1408]{2,1,0:T(8,128)} fusion(bf16[8,1024,4096]{2,1,0:T(8,128)(2,1)} %param.24, f32[4096]{0:T(1024)S(1)} %copy-done.22, f32[8,1024]{1,0:T(8,128)S(1)} %add_rsqrt_fusion, bf16[4096,1408]{1,0:T(8,128)(2,1)} %constant_dynamic-update-slice_fusion), kind=kOutput, calls=%fused_computation.18 | convolution fusion | flops 94623498240 | bytes 124829696 | tf_op jit(solution)/shard_map/bsd,de->bse/dot_general | solution.py:271
  176.6 6.8 copy.85
  183.4 7.3 reshape.188.bod_ref
  190.7 16.1 %reshape.176 = bf16[32,2,5,4,4096]{4,3,2,1,0:T(4,128)(2,1)} reshape(bf16[1280,4096]{1,0:T(8,128)(2,1)} %all-gather.4.cloned.1.call-done) | data formatting | bytes 20971520 | tf_op jit(solution)/shard_map/reshape | solution.py:260
  206.8 19.1 %copy.60 = bf16[32,2,5,4,4096]{4,1,3,0,2:T(2,128)(2,1)S(1)} copy(bf16[32,2,5,4,4096]{4,3,2,1,0:T(4,128)(2,1)} %reshape.176) | data formatting | bytes 20971520 | tf_op jit(solution)/shard_map/reshape | solution.py:260
  225.9 7.9 fusion.67
  233.8 5.0 mini-gather-slice.5
  241.0 9.3 gather_fusion.7
  250.3 4.3 copy.82
  254.6 9.7 gather_fusion.8
  264.3 4.0 copy.83
  268.3 8.5 gather_fusion.9
  276.8 59.9 %fusion.21 = bf16[8,1024,640]{2,1,0:T(8,128)(2,1)} fusion(bf16[8,640,1280]{2,1,0:T(8,128)(2,1)} %gather_fusion.9, bf16[8,640,1408]{2,1,0:T(8,128)(2,1)} %gather_fusion.8, bf16[8,640,1408]{2,1,0:T(8,128)(2,1)} %gather_fusion.7, bf16[8,1024,4096]{2,1,0:T(8,128)(2,1)} %param.24, f32[4096]{0:T(1024)S(1)} %copy-done.22, f32[8,1024]{1,0:T(8,128)S(1)} %add_rsqrt_fusion), kind=kOutput, calls=%fused_computation.37 | convolution fusion | flops 43214962688 | bytes 119586816 | tf_op jit(solution)/shard_map/bsd,brd->bsr/dot_general | solution.py:262
  336.7 5.8 fusion.26
  344.1 4.9 fusion.27
  348.9 4.3 fusion.28
  353.3 8.1 fusion.42
  361.3 22.0 %fusion.15 = bf16[8,1024,512]{2,1,0:T(8,128)(2,1)} fusion(f32[8,1024,1408]{2,1,0:T(8,128)} %fusion.6, f32[8,1024,512]{2,1,0:T(8,128)} %fusion.42, bf16[8,128,512]{2,1,0:T(8,128)(2,1)S(1)} %copy-done.12, bf16[8,1024,640]{2,1,0:T(8,128)(2,1)} %fusion.21), kind=kOutput, calls=%fused_computation.30 | convolution fusion | flops 1115684864 | bytes 61865984 | tf_op jit(solution)/shard_map/bsr,bre->bse/dot_general | solution.py:269
  383.4 7.1 convolution_convert_fusion
  390.4 52.0 %fusion.29 = f32[8,1024,4096]{2,1,0:T(8,128)} fusion(bf16[8,1024,512]{2,1,0:T(8,128)(2,1)} %fusion.15, bf16[512,4096]{1,0:T(8,128)(2,1)} %param.33), kind=kOutput, calls=%fused_computation.45 | convolution fusion | flops 34359738368 | bytes 146800640 | tf_op jit(solution)/shard_map/bsf,fd->bsd/dot_general | solution.py:284
  442.5 9.4 fusion.37
  453.3 15.7 %fusion.68 = f32[8,1024]{1,0:T(8,128)S(1)} fusion(pred[1024,1024]{0,1:T(8,128)(4,1)} %iota_compare_fusion, bf16[8,1024,64]{2,1,0:T(8,128)(2,1)} %get-tuple-element.11, bf16[8,1024,64]{2,1,0:T(8,128)(2,1)} %get-tuple-element.12, bf16[8,1024,64]{2,1,0:T(8,128)(2,1)} %get-tuple-element.8, bf16[8,1024,64]{2,1,0:T(8,128)(2,1)S(1)} %get-tuple-element.7), kind=kOutput, calls=%fused_computation.98 | convolution fusion | flops 2189427712 | bytes 5275648 | tf_op jit(solution)/shard_map/sub | solution.py:41
  468.9 20.6 %fusion.50 = bf16[8,128,1024]{2,1,0:T(8,128)(2,1)S(1)} fusion(bf16[8,1024,128]{2,1,0:T(8,128)(2,1)} %fusion.28, f32[8,1024]{1,0:T(8,128)S(1)} %fusion.68, pred[1024,1024]{0,1:T(8,128)(4,1)} %iota_compare_fusion, bf16[8,1024,64]{2,1,0:T(8,128)(2,1)} %get-tuple-element.11, bf16[8,1024,64]{2,1,0:T(8,128)(2,1)} %get-tuple-element.12, ...), kind=kOutput, calls=%fused_computation.69 | convolution fusion | flops 4346356736 | bytes 9469952 | tf_op jit(solution)/shard_map/bhqk,bkhd->bqhd/dot_general | solution.py:42
  491.2 2.4 pad_maximum_fusion.midp_ref
  493.6 65.2 %add_convert_fusion = bf16[8,1024,4096]{2,1,0:T(8,128)(2,1)} fusion(f32[8,1024,4096]{2,1,0:T(8,128)} %fusion.29, bf16[8,128,1024]{2,1,0:T(8,128)(2,1)S(1)} %fusion.50, bf16[1,128,4096]{2,1,0:T(8,128)(2,1)S(1)} %copy-done), kind=kOutput, calls=%fused_computation.16 | convolution fusion | flops 8657043456 | bytes 204472320 | tf_op jit(solution)/shard_map/bshe,hed->bsd/dot_general | solution.py:284
  558.8 486.2 %rsag.1 = bf16[8192,4096]{1,0:T(8,128)(2,1)} custom-call(s32[8]{0:T(128)} %ids_ref.1, bf16[8192,4096]{1,0:T(8,128)(2,1)} %bitcast.28.part_ref, bf16[8192,256]{1,0:T(8,128)(2,1)} %pad_maximum_fusion.midp_ref, bf16[8192,4096]{1,0:T(8,128)(2,1)} %bitcast.34.x_ref, bf16[2,256,4096]{2,1,0:T(8,128)(2,1)} %reshape.188.bod_ref), custom_call_target="tpu_custom_call" | custom-call | tf_op jit(solution)/shard_map/rsag/pallas_call | solution.py:226
  1045.0 44.5 %copy.95 = bf16[8,1024,4096]{2,1,0:T(8,128)(2,1)} copy(bf16[8,1024,4096]{2,1,0:T(8,128)(2,1)} %bitcast.37) | data formatting | bytes 134217728
  (76 shorter events, 28.5 us)
Async XLA Ops:
  6.5 487.0 %copy-start = (bf16[1,128,4096]{2,1,0:T(8,128)(2,1)S(1)}, bf16[1,128,4096]{2,1,0:T(8,128)(2,1)}, u32[]{:S(2)}) copy-start(bf16[1,128,4096]{2,1,0:T(8,128)(2,1)} %param.30) | copy-start | bytes 3145732
  6.6 170.0 %all-gather.6.cloned.1.call-start = ((), (), s32[]{:S(2)}) async-start(), calls=%async_computation.1 | async-start | bytes 4325376 | tf_op jit(solution)/shard_map/all_gather | solution.py:285
  8.2 182.5 %all-gather.4.cloned.1.call-start = ((), (), s32[]{:S(2)}) async-start(), calls=%async_computation | async-start | bytes 10813440 | tf_op jit(solution)/shard_map/all_gather | solution.py:259
  15.8 33.6 %copy-start.21 = (s32[1024]{0:T(1024)}, s32[1024]{0:T(1024)S(1)}, u32[]{:S(2)}) copy-start(s32[1024]{0:T(1024)S(1)} %pad_clamp_fusion) | copy-start | bytes 12292
  15.8 21.1 %copy-start.17 = (bf16[4096,1,128]{2,0,1:T(8,128)(2,1)S(1)}, bf16[4096,1,128]{2,0,1:T(8,128)(2,1)}, u32[]{:S(2)}) copy-start(bf16[4096,1,128]{2,0,1:T(8,128)(2,1)} %param.27) | copy-start | bytes 3145732
  15.8 22.3 %copy-start.13 = (bf16[2,128,1,128]{3,1,2,0:T(8,128)(2,1)S(1)}, bf16[2,128,1,128]{3,1,2,0:T(8,128)(2,1)}, u32[]{:S(2)}) copy-start(bf16[2,128,1,128]{3,1,2,0:T(8,128)(2,1)} %param.37) | copy-start | bytes 196612
  15.8 23.6 %copy-start.14 = (bf16[2,128,1,128]{3,1,2,0:T(8,128)(2,1)S(1)}, bf16[2,128,1,128]{3,1,2,0:T(8,128)(2,1)}, u32[]{:S(2)}) copy-start(bf16[2,128,1,128]{3,1,2,0:T(8,128)(2,1)} %param.35) | copy-start | bytes 196612
  36.8 6.7 copy-start.15
  36.8 8.0 copy-start.16
  36.8 9.3 copy-start.3
  36.8 10.9 copy-start.4
  38.1 11.3 %copy-start.5 = (bf16[2,512,128]{2,1,0:T(8,128)(2,1)S(1)}, bf16[2,512,128]{2,1,0:T(8,128)(2,1)}, u32[]{:S(2)}) copy-start(bf16[2,512,128]{2,1,0:T(8,128)(2,1)} %param.46) | copy-start | bytes 786436
  40.6 10.4 copy-start.18
  54.6 4.7 copy-start.6
  59.3 2.3 copy-start.22
  276.8 59.9 %copy-start.20 = (bf16[8,128,128]{2,1,0:T(8,128)(2,1)S(1)}, bf16[8,128,128]{2,1,0:T(8,128)(2,1)}, u32[]{:S(2)}) copy-start(bf16[8,128,128]{2,1,0:T(8,128)(2,1)} %gather_fusion.2) | copy-start | bytes 786436
  336.7 7.4 copy-start.1
  336.7 7.4 copy-start.19
  344.1 4.9 copy-start.10
  348.9 4.3 copy-start.2
  353.3 8.1 copy-start.12
  361.3 22.0 %copy-start.11 = (bf16[8,512,128]{2,1,0:T(8,128)(2,1)S(1)}, bf16[8,512,128]{2,1,0:T(8,128)(2,1)}, u32[]{:S(2)}) copy-start(bf16[8,512,128]{2,1,0:T(8,128)(2,1)} %gather_fusion.6) | copy-start | bytes 3145732
  451.9 1.4 copy-start.7
  468.9 20.6 %copy-start.9 = (bf16[8,128,128]{2,1,0:T(8,128)(2,1)S(1)}, bf16[8,128,128]{2,1,0:T(8,128)(2,1)}, u32[]{:S(2)}) copy-start(bf16[8,128,128]{2,1,0:T(8,128)(2,1)} %gather_fusion.5) | copy-start | bytes 786436
  489.6 1.6 copy-start.8
Sparse Core Ops, SparseCore 0:
  9.4 45.1 all-gather.5
  56.7 51.5 all-gather.3

commit v2 on v1

v2 whole, which is shorter than its diff:
```python
import functools
import math

import jax
import jax.numpy as jnp
from jax import lax
from jax.experimental import pallas as pl
from jax.experimental.pallas import tpu as pltpu
from jax.sharding import PartitionSpec as P

ALPHA = 16
EPS = 1e-5
ROPE_BASE = 10000.0
MESH = pl.DeviceIdType.MESH
BF = jnp.bfloat16

def fused_kernel(cfg, ids_ref, x_ref, h_ref, at_ref, wq_ref, wk_ref, wv_ref, wg_ref, wu_ref, wo_ref, wd_ref, bqk_ref, bv_ref, bgu_ref,
                 aod_ref, bown_ref, cos_ref, sin_ref, stage_ref,
                 hbuf, mids, at_v, wqkv_v, wgu_v, wod_v, bqk_v, bv_v, bgu_v, aod_v, bod_v, cos_v, sin_v, qbuf, kbuf, vbuf, om,
                 psend, l0, r0, l1f, l1d, l1s, s1, r1, l2f, l2d, l2s, s2, r2, xrow, yrow,
                 w_sem, x_sem, d2d_s, d2d_r, p1_s, p1_r, p2_s, p2_r, aga_s, aga_r, agb_s, agb_r, dd_s, dd_r, bg_s, bg_r, loc_sem):
    R, NT, TT, W, D, HEAD, FF, scale, tps = cfg
    HALF = TT // 2
    B1 = HALF // R
    B2 = B1 // R
    WH = W // 2
    DH = D // 2
    KV = tps * TT
    FB = HALF
    idx = lax.axis_index("tensor")
    c = lax.rem(idx, 2)
    xx = lax.rem(idx // 2, R)
    yy = idx // (2 * R)
    q1 = jnp.where(c == 0, xx, yy)
    q2 = jnp.where(c == 0, yy, xx)
    st1 = 2 + (2 * R - 2) * c
    st2 = 2 * R - (2 * R - 2) * c
    base1 = idx - q1 * st1
    base2 = idx - q2 * st2
    plus1 = base1 + lax.rem(q1 + 1, R) * st1
    minus1 = base1 + lax.rem(q1 + R - 1, R) * st1
    plus2 = base2 + lax.rem(q2 + 1, R) * st2
    minus2 = base2 + lax.rem(q2 + R - 1, R) * st2
    mate = idx + 1 - 2 * c
    peers = (mate, plus1, minus1, plus2, minus2)

    resident = (
        ((at_ref, at_v),),
        ((wq_ref, wqkv_v.at[:, pl.ds(0, HEAD)]), (wk_ref, wqkv_v.at[:, pl.ds(HEAD, HEAD)]), (wv_ref, wqkv_v.at[:, pl.ds(2 * HEAD, HEAD)]),
         (bqk_ref, bqk_v), (bv_ref, bv_v), (cos_ref, cos_v), (sin_ref, sin_v)),
        ((wg_ref.at[:, pl.ds(0, FB)], wgu_v.at[:, pl.ds(0, FB)]), (wu_ref.at[:, pl.ds(0, FB)], wgu_v.at[:, pl.ds(FB, FB)]),
         (wg_ref.at[:, pl.ds(FB, FB)], wgu_v.at[:, pl.ds(2 * FB, FB)]), (wu_ref.at[:, pl.ds(FB, FB)], wgu_v.at[:, pl.ds(3 * FB, FB)]),
         (bgu_ref, bgu_v)),
        ((wo_ref, wod_v.at[pl.ds(0, HEAD), :]), (wd_ref, wod_v.at[pl.ds(HEAD, FF), :]), (aod_ref, aod_v)),
    )
    copies = []
    n_sem = 0
    for group in resident:
        row = []
        for src, dst in group:
            row.append(pltpu.make_async_copy(src, dst, w_sem.at[n_sem]))
            n_sem += 1
        copies.append(row)

    def xcopy(u):
        rows = pl.ds(pl.multiple_of(u * HALF, HALF), HALF)
        s = lax.rem(u, 2)
        return pltpu.make_async_copy(h_ref.at[rows, :], hbuf.at[s], x_sem.at[s])

    CB = bown_ref.shape[-1]

    def bcols(d):
        return pl.ds(pl.multiple_of(d * CB, CB), CB)

    bown = pltpu.make_async_copy(bown_ref, bod_v.at[:, :, bcols(idx)], loc_sem.at[2])
    xcopy(0).start()
    for row in copies:
        for cp in row:
            cp.start()

    bown.start()

    bar = pltpu.get_barrier_semaphore()
    for p in peers:
        pl.semaphore_signal(bar, inc=1, device_id={"tensor": p}, device_id_type=MESH)
    pl.semaphore_wait(bar, len(peers))
    vbuf[...] = jnp.zeros_like(vbuf)
    kbuf[...] = jnp.zeros_like(kbuf)

    def settle(t, hf, k):
        if hf == 0:
            @pl.when(t == 0)
            def _():
                for cp in copies[k]:
                    cp.wait()

    def rc(src, dst, ss, rs, dev):
        return pltpu.make_async_remote_copy(src_ref=src, dst_ref=dst, send_sem=ss, recv_sem=rs, device_id={"tensor": dev}, device_id_type=MESH)

    def blk(q, d, rows):
        return pl.ds(pl.multiple_of(lax.rem(q + d + R, R) * rows, rows), rows)

    A, B = pl.ds(0, WH), pl.ds(WH, WH)
    DA, DB = pl.ds(0, DH), pl.ds(DH, DH)

    def d2d(t):
        s = lax.rem(t, 2)
        return rc(psend, l0.at[s], d2d_s, d2d_r.at[s], mate)

    def first_copies(src, q, rows, lf, ld, ss, rs, plus, minus):
        return (rc(src.at[blk(q, 2, rows), A], lf.at[0], ss.at[0], rs.at[0], plus),
                rc(src.at[blk(q, 2, rows), B], lf.at[1], ss.at[1], rs.at[1], minus),
                rc(src.at[blk(q, 1, rows), B], ld.at[0], ss.at[2], rs.at[2], plus),
                rc(src.at[blk(q, -1, rows), A], ld.at[1], ss.at[3], rs.at[3], minus))

    def second_copies(sm, ls, ss, rs, plus, minus):
        return (rc(sm.at[0], ls.at[0], ss.at[4], rs.at[4], plus),
                rc(sm.at[1], ls.at[1], ss.at[5], rs.at[5], minus))

    def p1s1(t):
        return first_copies(r0, q1, B1, l1f, l1d, p1_s, p1_r, plus1, minus1)

    def p1s2(t):
        return second_copies(s1, l1s, p1_s, p1_r, plus1, minus1)

    def p2s1(t):
        s = lax.rem(t, 2)
        return first_copies(r1.at[s], q2, B2, l2f.at[s], l2d.at[s], p2_s.at[s], p2_r.at[s], plus2, minus2)

    def p2s2(t):
        s = lax.rem(t, 2)
        return second_copies(s2, l2s.at[s], p2_s.at[s], p2_r.at[s], plus2, minus2)

    def row0(t):
        return t * TT + c * HALF

    def rows_a(t, d):
        return pl.ds(pl.multiple_of(row0(t) + q1 * B1 + lax.rem(q2 + d + R, R) * B2, B2), B2)

    def rows_b(t, d):
        return pl.ds(pl.multiple_of(row0(t) + lax.rem(q1 + d + R, R) * B1, B1), B1)

    def same(rows, cols, ss, rs, dev):
        return rc(stage_ref.at[rows, cols], stage_ref.at[rows, cols], ss, rs, dev)

    def sl(t):
        return lax.rem(t, 4)

    def aga1(t):
        s, r = sl(t), rows_a(t, 0)
        return (rc(yrow, stage_ref.at[r, :], aga_s.at[s, 0], aga_r.at[s, 0], plus2),
                rc(yrow, stage_ref.at[r, :], aga_s.at[s, 1], aga_r.at[s, 1], minus2))

    def aga2(t):
        s = sl(t)
        return (same(rows_a(t, -1), DA, aga_s.at[s, 2], aga_r.at[s, 2], plus2),
                same(rows_a(t, 1), DB, aga_s.at[s, 3], aga_r.at[s, 3], minus2))

    def agb1(t):
        s, r = sl(t), rows_b(t, 0)
        return (same(r, pl.ds(0, D), agb_s.at[s, 0], agb_r.at[s, 0], plus1),
                same(r, pl.ds(0, D), agb_s.at[s, 1], agb_r.at[s, 1], minus1))

    def agb2(t):
        s = sl(t)
        return (same(rows_b(t, -1), DA, agb_s.at[s, 2], agb_r.at[s, 2], plus1),
                same(rows_b(t, 1), DB, agb_s.at[s, 3], agb_r.at[s, 3], minus1))

    def dd(t):
        s, r = sl(t), pl.ds(pl.multiple_of(row0(t), HALF), HALF)
        return same(r, pl.ds(0, D), dd_s.at[s], dd_r.at[s], mate)

    def yloc(t):
        return pltpu.make_async_copy(yrow, stage_ref.at[rows_a(t, 0), :], loc_sem.at[0])

    def xload(t):
        return pltpu.make_async_copy(x_ref.at[rows_a(t, 0), :], xrow, loc_sem.at[1])

    def start(cs):
        for cp in cs:
            cp.start()

    def wrecv(cs):
        for cp in cs:
            cp.wait_recv()

    def wsend(cs):
        for cp in cs:
            cp.wait_send()

    def comb(src, q, rows, lf, ld, sm, dst):
        sm[0] = src[blk(q, 1, rows), A] + lf[0]
        sm[1] = src[blk(q, -1, rows), B] + lf[1]
        dst[:, A] = src[blk(q, 0, rows), A] + ld[1]
        dst[:, B] = src[blk(q, 0, rows), B] + ld[0]

    def e1(t):
        wrecv(p1s1(t))
        wsend(p1s1(t))

        @pl.when(t >= 1)
        def _():
            wsend(p1s2(t - 1))
        comb(r0, q1, B1, l1f, l1d, s1, r1.at[lax.rem(t, 2)])
        start(p1s2(t))

    def e2(t):
        s = lax.rem(t, 2)
        wrecv(p1s2(t))
        r1[s, :, A] = r1[s, :, A] + l1s[0]
        r1[s, :, B] = r1[s, :, B] + l1s[1]
        start(p2s1(t))

    def e3(t):
        s = lax.rem(t, 2)
        wrecv(p2s1(t))
        wsend(p2s1(t))

        @pl.when(t >= 1)
        def _():
            wsend(p2s2(t - 1))
        comb(r1.at[s], q2, B2, l2f.at[s], l2d.at[s], s2, r2)
        start(p2s2(t))
        xload(t).start()

    def e4(t):
        s = lax.rem(t, 2)
        wrecv(p2s2(t))
        xload(t).wait()
        i = ids_ref[t // tps]
        r2[:, A] = r2[:, A] + l2s[s, 0]
        r2[:, B] = r2[:, B] + l2s[s, 1]
        lor = jnp.dot(r2[:, pl.ds(D, W - D)], bod_v[i], preferred_element_type=jnp.float32)
        y = xrow[...].astype(jnp.float32) + r2[:, pl.ds(0, D)].astype(jnp.float32) + scale * lor
        yrow[...] = y.astype(BF)
        yloc(t).start()
        start(aga1(t))

    def e5(t):
        yloc(t).wait()
        wsend(aga1(t))
        wrecv(aga1(t))
        start(aga2(t))

    def e6(t):
        wrecv(aga2(t))
        start(agb1(t))

    def e7(t):
        wrecv(agb1(t))
        start(agb2(t))

    def e8(t):
        wrecv(agb2(t))
        start((dd(t),))

    def e9(t):
        wrecv((dd(t),))
        wsend((dd(t),))
        wsend(agb2(t))
        wsend(agb1(t))
        wsend(aga2(t))

    F32 = jnp.float32

    def pa(t, hf):
        u = 2 * t + hf
        settle(t, hf, 0)
        xcopy(u).wait()

        @pl.when(u + 1 < 2 * NT)
        def _():
            xcopy(u + 1).start()
        i = ids_ref[t // tps]
        mids[...] = lax.dot_general(hbuf[hf], at_v[i], (((1,), (1,)), ((), ())), preferred_element_type=F32).astype(BF)

    def rope(z, rows):
        return z * cos_v[rows, :] + pltpu.roll(z, HEAD // 2, 1) * sin_v[rows, :]

    def pb(t, hf):
        settle(t, hf, 1)
        i = ids_ref[t // tps]
        pos = pl.ds(pl.multiple_of(lax.rem(t, tps) * TT + hf * HALF, HALF), HALF)
        z = jnp.dot(hbuf[hf], wqkv_v[...], preferred_element_type=F32)
        lqk = jnp.dot(mids[:, pl.ds(0, 2 * HEAD)], bqk_v[i], preferred_element_type=F32)
        lv = jnp.dot(mids[:, pl.ds(2 * HEAD, 2 * HEAD)], bv_v[i], preferred_element_type=F32)
        qbuf[...] = rope(z[:, :HEAD] + scale * lqk[:, :HEAD], pos).astype(BF)
        kbuf[pos, :] = rope(z[:, HEAD:2 * HEAD] + scale * lqk[:, HEAD:], pos).astype(BF)
        vbuf[pos, :] = (z[:, 2 * HEAD:] + scale * lv).astype(BF)

    def pc(t, hf):
        settle(t, hf, 2)
        i = ids_ref[t // tps]
        for n in range(FF // FB):
            cols = pl.ds(n * 2 * FB, 2 * FB)
            z = jnp.dot(hbuf[hf], wgu_v[:, cols], preferred_element_type=F32)
            z = z + scale * jnp.dot(mids[:, pl.ds(4 * HEAD, 2 * HEAD)], bgu_v[i, :, cols], preferred_element_type=F32)
            g = z[:, :FB]
            om[lax.rem(t, 2), hf, :, pl.ds(HEAD + n * FB, FB)] = (g * (1.0 / (1.0 + jnp.exp(-g))) * z[:, FB:]).astype(BF)

    def pd(t, hf):
        sc = lax.dot_general(qbuf[...], kbuf[...], (((1,), (1,)), ((), ())), preferred_element_type=F32) * (1.0 / math.sqrt(HEAD))
        row = lax.rem(t, tps) * TT + hf * HALF + lax.broadcasted_iota(jnp.int32, (HALF, KV), 0)
        col = lax.broadcasted_iota(jnp.int32, (HALF, KV), 1)
        sc = jnp.where(row >= col, sc, -1e30)
        e = jnp.exp(sc - jnp.max(sc, axis=-1, keepdims=True))
        p = (e / jnp.sum(e, axis=-1, keepdims=True)).astype(BF)
        om[lax.rem(t, 2), hf, :, pl.ds(0, HEAD)] = jnp.dot(p, vbuf[...], preferred_element_type=F32).astype(BF)

    def out_proj(t, half, dst, extra):
        i = ids_ref[t // tps]
        act = om[lax.rem(t, 2), half]
        last = jnp.dot(act, aod_v[i], preferred_element_type=F32)
        tail = pl.ds(D, W - D)
        dst[:, tail] = (last if extra is None else last + extra[:, tail].astype(F32)).astype(BF)
        NB = 512
        for n in range(D // NB):
            cols = pl.ds(n * NB, NB)
            acc = jnp.dot(act, wod_v[:, cols], preferred_element_type=F32)
            dst[:, cols] = (acc if extra is None else acc + extra[:, cols].astype(F32)).astype(BF)

    def pf(t):
        settle(t, 0, 3)

        @pl.when(t >= 1)
        def _():
            d2d(t - 1).wait_send()
        out_proj(t, 1 - c, psend, None)
        d2d(t).start()

    def pg(t):
        d2d(t).wait_recv()
        out_proj(t, c, r0, l0.at[lax.rem(t, 2)])
        start(p1s1(t))

    def guard(t, f, *a):
        @pl.when(jnp.logical_and(t >= 0, t < NT))
        def _():
            f(t, *a)

    def piece(ad, d, k, dev):
        ref = bod_v.at[ad, :, bcols(d)] if ad is not None else bod_v.at[:, :, bcols(d)]
        return rc(ref, ref, bg_s.at[k], bg_r.at[k], dev)

    def line(dev, k):
        return dev + (k - q2) * st2

    def g1():
        return (piece(None, idx, 0, plus2), piece(None, idx, 1, minus2))

    def g2():
        return (piece(0, minus2, 2, plus2), piece(1, plus2, 3, minus2))

    def g3():
        return tuple(piece(None, line(idx, k), 4 + k, plus1) for k in range(R)) + tuple(piece(None, line(idx, k), 4 + R + k, minus1) for k in range(R))

    def g4():
        return tuple(piece(0, line(minus1, k), 4 + 2 * R + k, plus1) for k in range(R)) + tuple(piece(1, line(plus1, k), 4 + 3 * R + k, minus1) for k in range(R))

    def g5():
        return tuple(piece(None, 2 * j + c, 4 + 4 * R + j, mate) for j in range(R * R))

    def b1():
        bown.wait()
        start(g1())

    def b2():
        wrecv(g1())
        start(g2())

    def b3():
        wrecv(g2())
        start(g3())

    def b4():
        wrecv(g3())
        start(g4())

    def b5():
        wrecv(g4())
        start(g5())

    def b6():
        for g in (g1, g2, g3, g4, g5):
            wsend(g())
        wrecv(g5())

    def at_step(it, k, f):
        @pl.when(it == k)
        def _():
            f()

    b1()

    def body(it, _):
        guard(it, pa, 0)
        guard(it, pb, 0)
        at_step(it, 0, b2)
        at_step(it, 1, b4)
        at_step(it, 3, b6)
        guard(it - 5, e7)
        guard(it - 4, e5)
        guard(it - 3, e4)
        guard(it - 2, e2)
        guard(it - 1, pg)
        guard(it, pc, 0)
        guard(it, pd, 0)
        guard(it, pa, 1)
        guard(it, pb, 1)
        at_step(it, 0, b3)
        at_step(it, 1, b5)
        guard(it - 1, e1)
        guard(it - 2, e3)
        guard(it - 4, e6)
        guard(it - 5, e8)
        guard(it - 6, e9)
        guard(it, pc, 1)
        guard(it, pd, 1)
        guard(it, pf)
        return 0
    lax.fori_loop(0, NT + 6, body, 0)
    last = NT - 1
    d2d(last).wait_send()
    wsend(p1s2(last))
    wsend(p2s2(last))


def fused(mesh, ids, x, h, at, wq, wk, wv, wg, wu, wo, wd, bqk, bv, bgu, aod, bown, cos, sin, scale, seq_len, TT):
    R = math.isqrt(mesh.shape["tensor"] // 2)
    T, D = x.shape
    HEAD, FF = wo.shape[0], wd.shape[0]
    W = D + aod.shape[-1]
    NT, HALF = T // TT, TT // 2
    B1 = HALF // R
    B2 = B1 // R
    WH = W // 2
    cfg = (R, NT, TT, W, D, HEAD, FF, scale, seq_len // TT)
    S = pltpu.SemaphoreType.DMA

    def V(*shape):
        return pltpu.VMEM(shape, BF)
    n_in = 17
    return pl.pallas_call(
        functools.partial(fused_kernel, cfg), name="block",
        out_shape=jax.ShapeDtypeStruct((T, D), BF),
        in_specs=[pl.BlockSpec(memory_space=pltpu.SMEM)] + [pl.BlockSpec(memory_space=pltpu.HBM)] * n_in,
        out_specs=pl.BlockSpec(memory_space=pltpu.HBM),
        scratch_shapes=[V(2, HALF, D), V(HALF, at.shape[1]), V(*at.shape), V(D, 3 * HEAD), V(D, 2 * FF), V(HEAD + FF, D),
                        V(*bqk.shape), V(*bv.shape), V(*bgu.shape), V(*aod.shape), V(*bown.shape[:2], D),
                        pltpu.VMEM(cos.shape, jnp.float32), pltpu.VMEM(sin.shape, jnp.float32), V(HALF, HEAD), V(seq_len, HEAD), V(seq_len, HEAD), V(2, 2, HALF, HEAD + FF),
                        V(HALF, W), V(2, HALF, W), V(HALF, W),
                        V(2, B1, WH), V(2, B1, WH), V(2, B1, WH), V(2, B1, WH), V(2, B1, W),
                        V(2, 2, B2, WH), V(2, 2, B2, WH), V(2, 2, B2, WH), V(2, B2, WH), V(B2, W),
                        V(B2, D), V(B2, D),
                        S((17,)), S((2,)), S, S((2,)), S((6,)), S((6,)), S((2, 6)), S((2, 6)), S((4, 4)), S((4, 4)), S((4, 4)), S((4, 4)), S((4,)), S((4,)), S((4 + 4 * R + R * R,)), S((4 + 4 * R + R * R,)), S((3,))],
        compiler_params=pltpu.CompilerParams(collective_id=0, has_side_effects=True, vmem_limit_bytes=67043328),
    )(ids, x, h, at, wq, wk, wv, wg, wu, wo, wd, bqk, bv, bgu, aod, bown, cos, sin)


def norm_kernel(x_ref, gain_ref, h_ref):
    rows_per = 16
    dim = x_ref.shape[1]

    def step(k, _):
        rows = pl.ds(pl.multiple_of(k * rows_per, rows_per), rows_per)
        xf = x_ref[rows, :].astype(jnp.float32)
        inv = lax.rsqrt(jnp.sum(xf * xf, axis=-1, keepdims=True) * (1.0 / dim) + EPS)
        h_ref[rows, :] = (xf * inv * gain_ref[...]).astype(BF)
        return 0
    lax.fori_loop(0, x_ref.shape[0] // rows_per, step, 0, unroll=4)


def norm(x, gain):
    T, D = x.shape
    rows = 256
    return pl.pallas_call(
        norm_kernel, name="norm", grid=(T // rows,),
        out_shape=jax.ShapeDtypeStruct((T, D), BF),
        in_specs=[pl.BlockSpec((rows, D), lambda i: (i, 0)), pl.BlockSpec((1, D), lambda i: (0, 0))],
        out_specs=pl.BlockSpec((rows, D), lambda i: (i, 0)),
        cost_estimate=pl.CostEstimate(flops=8000 * T * D // 1000 * 1000, bytes_accessed=4 * T * D, transcendentals=0),
    )(x, gain)


def solution(mesh):
    batch_spec = P('data', None, None)
    head_cols = P(None, 'tensor', None)
    head_rows = P('tensor', None, None)
    ff_cols = P(None, 'tensor')
    ff_rows = P('tensor', None)
    last_split = P(None, None, 'tensor')
    b_heads = P(None, None, 'tensor', None)
    a_heads = P(None, 'tensor', None, None)
    in_specs = (batch_spec, P('data'), P(None), head_cols, head_cols, head_cols, head_rows, ff_cols, ff_cols, ff_rows, last_split, b_heads, last_split, b_heads, last_split, b_heads, a_heads, last_split, last_split, last_split, last_split, last_split, head_cols, last_split)

    def local_layer(x_blk, adapter_ids, norm_gain, w_query, w_key, w_value, w_out, w_gate, w_up, w_down, a_query, b_query, a_key, b_key, a_value, b_value, a_out, b_out, a_gate, b_gate, a_up, b_up, a_down, b_down):
        seq_len = x_blk.shape[1]
        rank = a_out.shape[-1]
        scale = ALPHA / rank
        n_dev = mesh.shape['tensor']
        dim = x_blk.shape[2]
        n_ad = a_query.shape[0]
        zero_a = jnp.zeros_like(a_value)
        mine = jnp.concatenate([a_query, a_key, a_value, zero_a, a_gate, a_up], axis=2)
        mine = jnp.transpose(mine, (0, 2, 1)).reshape(n_ad * 3, -1, dim)
        a_all = lax.all_gather(mine, 'tensor', axis=1, tiled=True)
        a_all = a_all.reshape(n_ad, -1, dim)
        b_own = jnp.concatenate([b_out, b_down], axis=1)
        x_flat = x_blk.reshape(-1, dim)
        normed = norm(x_flat, norm_gain.reshape(1, dim))

        def weave(b_first, b_second):
            first = b_first.reshape(n_ad, n_dev, rank // n_dev, -1)
            second = b_second.reshape(n_ad, n_dev, rank // n_dev, -1)
            return first, second

        def pair(b_first, b_second):
            first, second = weave(b_first, b_second)
            zf, zs = jnp.zeros_like(first), jnp.zeros_like(second)
            rows = jnp.concatenate([jnp.concatenate([first, zs], axis=3), jnp.concatenate([zf, second], axis=3)], axis=2)
            return rows.reshape(n_ad, 2 * rank, -1)

        head = w_query.shape[-1]
        ff = w_gate.shape[1]
        tile = seq_len // 2
        fb = tile // 2
        bqk = pair(b_query, b_key)
        bv_first, _ = weave(b_value, b_value)
        bv = jnp.concatenate([bv_first, jnp.zeros_like(bv_first)], axis=2).reshape(n_ad, 2 * rank, -1)
        bgu = pair(b_gate, b_up).reshape(n_ad, 2 * rank, 2, ff // fb, fb)
        bgu = jnp.transpose(bgu, (0, 1, 3, 2, 4)).reshape(n_ad, 2 * rank, 2 * ff)
        ao = a_out.reshape(n_ad, head, rank)
        aod = jnp.concatenate([jnp.concatenate([ao, jnp.zeros_like(ao)], axis=2), jnp.concatenate([jnp.zeros_like(a_down), a_down], axis=2)], axis=1)
        half = head // 2
        inv_freq = ROPE_BASE ** (-jnp.arange(half, dtype=jnp.float32) / half)
        angles = jnp.arange(seq_len, dtype=jnp.float32)[:, None] * inv_freq[None, :]
        cos_t, sin_t = jnp.cos(angles), jnp.sin(angles)
        cos_t = jnp.concatenate([cos_t, cos_t], axis=1)
        sin_t = jnp.concatenate([-sin_t, sin_t], axis=1)
        out = fused(mesh, adapter_ids, x_flat, normed, a_all, w_query.reshape(dim, head), w_key.reshape(dim, head), w_value.reshape(dim, head),
                    w_gate, w_up, w_out.reshape(head, dim), w_down, bqk, bv, bgu, aod, b_own, cos_t, sin_t, scale, seq_len, tile)
        return out.reshape(x_blk.shape)

    return jax.shard_map(local_layer, mesh=mesh, in_specs=in_specs, out_specs=batch_spec, check_vma=False)
```

time: 1110 us -> 650 us (0.59); the launches traced: 1100 us -> 650 us
  matrix products: 381 us -> 0 us
  local copies, waits for them, and re-layouts: 176 us -> 55.4 us
  Pallas kernels: 486 us -> 575 us
  other arithmetic: 39.4 us -> 5.99 us
    dot_general x12 -> x0, matrix products: 366 us -> none  [the longest x1 115 us: local_layer(): jnp.einsum('bsd,de->bse', normed, w_in, preferred_element_type=jnp.float32)]
    pallas_call x1 -> x2, Pallas kernels: 486 us -> 575 us  [the longest x1 508 us: fused(): pl.pallas_call(functools.partial(fused_kernel, cfg), name='block', out_sh...]
    gather x12 -> x0, local copies, waits for them, and re-layouts: 50.5 us -> none  [the longest x5 40.4 us: local_layer(): a_all[adapter_ids]]
    reshape x4, local copies, waits for them, and re-layouts: 43.3 us -> 4.18 us  [the longest x1 1.59 us: local_layer(): bgu = jnp.transpose(bgu, (0, 1, 3, 2, 4)).reshape(n_ad, 2 * rank, 2 * ff)]
    unnamed x58 -> x15, local copies, waits for them, and re-layouts: 71.7 us -> 44.5 us
    reduce_sum x1 -> x0, other arithmetic: 21 us -> none  [rms_norm(): jnp.mean(x_f32 * x_f32, axis=-1, keepdims=True) + EPS]
    sub x1 -> x0, matrix products: 15.7 us -> none  [causal_attention(): jax.nn.softmax(jnp.where(causal, scores, -1e+30), axis=-1)]
  transfers between devices with their start and end apart: 2 -> 1, of which waited for: 0 -> 0; matrix products, arithmetic and copies ran while one was open for 17% -> 2% of each run, Pallas kernels for 0% -> 10%
where the time goes in v2:
time: 650 us
  Pallas kernels  575 us (88%)
  local copies, waits for them, and re-layouts  55.4 us (9%)
  between operations  13.5 us (2%)
    pallas_call x1, Pallas kernels, fused(): pl.pallas_call(functools.partial(fused_kernel, cfg), name='block', out_sh...  508 us
    pallas_call x1, Pallas kernels, norm(): pl.pallas_call(norm_kernel, name='norm', grid=(T // rows,), out_shape=jax...  66.5 us
    unnamed x15, local copies, waits for them, and re-layouts  44.5 us
  transfers between devices with their start and end apart: 1, of which 0 were waited for; matrix products, arithmetic and copies ran while one was open for 2% of the time, Pallas kernels for 10%

profile of v2, /device:TPU:97, one launch (start us, length us, event | category | flops | bytes accessed | tf_op | source)
XLA Modules:
  0.0 649.6 jit_solution(8526255316129123296)
XLA Ops:
  6.5 0.0 copy-start
  6.5 0.0 all-gather.2.cloned.1.call-start
  6.6 4.8 concatenate.42
  11.4 0.1 all-gather.2.cloned.1.call-update
  11.5 1.5 pad_bitcast_fusion.bv_ref
  13.0 1.0 reshape.73
  14.0 0.0 copy-done
  14.0 0.1 reshape.74
  14.1 0.4 fusion.4
  14.5 0.8 reshape_reshape.3
  15.3 1.1 copy.25
  16.4 0.0 copy-start.2
  16.4 0.0 copy-start.3
  16.4 0.0 copy-start.4
  16.4 0.0 copy-start.5
  16.4 0.0 copy-start.1
  16.4 0.0 copy-start.6
  16.4 1.6 reshape.75.bgu_ref
  18.0 2.0 fusion.12
  20.0 0.0 copy-done.2
  20.0 0.0 copy-done.3
  20.0 0.6 pad_maximum_fusion.2.bown_ref
  20.6 0.0 copy-done.4
  20.6 0.0 copy-done.5
  20.6 0.8 fusion.11.bqk_ref
  21.4 0.0 copy-done.1
  21.5 0.0 copy-done.6
  21.5 0.9 fusion.5.aod_ref
  22.4 1.3 pad_maximum_fusion
  23.7 66.5 %norm.1.h_ref = bf16[8192,4096]{1,0:T(8,128)(2,1)} custom-call(bf16[8192,4096]{1,0:T(8,128)(2,1)} %bitcast.x_ref, f32[1,4096]{1,0:T(1,128)} %bitcast.33), custom_call_target="tpu_custom_call" | custom-call | flops 268435456000 | bytes 134217728 | tf_op jit(solution)/shard_map/norm/pallas_call | solution.py:476
  90.2 508.1 %block.1 = bf16[8192,4096]{1,0:T(8,128)(2,1)} custom-call(s32[8]{0:T(128)} %ids_ref.1, bf16[8192,4096]{1,0:T(8,128)(2,1)} %bitcast.x_ref, bf16[8192,4096]{1,0:T(8,128)(2,1)} %norm.1.h_ref, bf16[2,768,4096]{2,1,0:T(8,128)(2,1)} %bitcast.22, bf16[4096,128]{1,0:T(8,128)(2,1)} %bitcast.25, bf16[4096,128]{1,0:T(8,128)(2,1)} %bitcast.26, ...), custom_call_target="tpu_custom_call" | custom-call | tf_op jit(solution)/shard_map/block/pallas_call | solution.py:443
  598.3 44.5 %copy.27 = bf16[8,1024,4096]{2,1,0:T(8,128)(2,1)} copy(bf16[8,1024,4096]{2,1,0:T(8,128)(2,1)} %bitcast.16) | data formatting | bytes 134217728
  (3 shorter events, 0.0 us)
Async XLA Ops:
  6.5 7.5 %copy-start = (bf16[2,128,512]{2,1,0:T(8,128)(2,1)S(1)}, bf16[2,128,512]{2,1,0:T(8,128)(2,1)}, u32[]{:S(2)}) copy-start(bf16[2,128,512]{2,1,0:T(8,128)(2,1)} %param.45) | copy-start | bytes 786436
  6.5 83.6 %all-gather.2.cloned.1.call-start = ((), (), s32[]{:S(2)}) async-start(), calls=%async_computation | async-start | bytes 12976128 | tf_op jit(solution)/shard_map/all_gather | solution.py:506
  16.4 3.6 copy-start.2
  16.4 3.6 copy-start.3
  16.4 4.3 copy-start.4
  16.4 4.3 copy-start.5
  16.4 5.0 copy-start.1
  16.4 5.0 copy-start.6
Sparse Core Ops, SparseCore 0:
  11.6 61.5 all-gather.1

commit v3 on v2

--- a/solution.py
+++ b/solution.py
@@ -3,6 +3,7 @@
 
 import jax
 import jax.numpy as jnp
+import numpy as np
 from jax import lax
 from jax.experimental import pallas as pl
 from jax.experimental.pallas import tpu as pltpu
@@ -14,11 +15,11 @@
 MESH = pl.DeviceIdType.MESH
 BF = jnp.bfloat16
 
-def fused_kernel(cfg, ids_ref, x_ref, h_ref, at_ref, wq_ref, wk_ref, wv_ref, wg_ref, wu_ref, wo_ref, wd_ref, bqk_ref, bv_ref, bgu_ref,
-                 aod_ref, bown_ref, cos_ref, sin_ref, stage_ref,
-                 hbuf, mids, at_v, wqkv_v, wgu_v, wod_v, bqk_v, bv_v, bgu_v, aod_v, bod_v, cos_v, sin_v, qbuf, kbuf, vbuf, om,
+def fused_kernel(cfg, ids_ref, x_ref, gain_ref, aown_ref, wq_ref, wk_ref, wv_ref, wg_ref, wu_ref, wo_ref, wd_ref, bin_ref, ao_ref, ad_ref,
+                 bown_ref, cos_ref, sin_ref, stage_ref,
+                 xbuf, hbuf, mids, gain_v, at_v, wqkv_v, wgu_v, wod_v, bin_v, aod_v, bod_v, cos_v, sin_v, qbuf, kbuf, vbuf, om,
                  psend, l0, r0, l1f, l1d, l1s, s1, r1, l2f, l2d, l2s, s2, r2, xrow, yrow,
-                 w_sem, x_sem, d2d_s, d2d_r, p1_s, p1_r, p2_s, p2_r, aga_s, aga_r, agb_s, agb_r, dd_s, dd_r, bg_s, bg_r, loc_sem):
+                 w_sem, x_sem, d2d_s, d2d_r, p1_s, p1_r, p2_s, p2_r, aga_s, aga_r, agb_s, agb_r, dd_s, dd_r, ag_s, ag_r, bg_s, bg_r, loc_sem):
     R, NT, TT, W, D, HEAD, FF, scale, tps = cfg
     HALF = TT // 2
     B1 = HALF // R
@@ -27,6 +28,8 @@
     DH = D // 2
     KV = tps * TT
     FB = HALF
+    RANK = (W - D) // 2
+    AR = aown_ref.shape[1]
     idx = lax.axis_index("tensor")
     c = lax.rem(idx, 2)
     xx = lax.rem(idx // 2, R)
@@ -45,13 +48,12 @@
     peers = (mate, plus1, minus1, plus2, minus2)
 
     resident = (
-        ((at_ref, at_v),),
+        ((gain_ref, gain_v),),
         ((wq_ref, wqkv_v.at[:, pl.ds(0, HEAD)]), (wk_ref, wqkv_v.at[:, pl.ds(HEAD, HEAD)]), (wv_ref, wqkv_v.at[:, pl.ds(2 * HEAD, HEAD)]),
-         (bqk_ref, bqk_v), (bv_ref, bv_v), (cos_ref, cos_v), (sin_ref, sin_v)),
+         (bin_ref, bin_v), (cos_ref, cos_v), (sin_ref, sin_v)),
         ((wg_ref.at[:, pl.ds(0, FB)], wgu_v.at[:, pl.ds(0, FB)]), (wu_ref.at[:, pl.ds(0, FB)], wgu_v.at[:, pl.ds(FB, FB)]),
-         (wg_ref.at[:, pl.ds(FB, FB)], wgu_v.at[:, pl.ds(2 * FB, FB)]), (wu_ref.at[:, pl.ds(FB, FB)], wgu_v.at[:, pl.ds(3 * FB, FB)]),
-         (bgu_ref, bgu_v)),
-        ((wo_ref, wod_v.at[pl.ds(0, HEAD), :]), (wd_ref, wod_v.at[pl.ds(HEAD, FF), :]), (aod_ref, aod_v)),
+         (wg_ref.at[:, pl.ds(FB, FB)], wgu_v.at[:, pl.ds(2 * FB, FB)]), (wu_ref.at[:, pl.ds(FB, FB)], wgu_v.at[:, pl.ds(3 * FB, FB)])),
+        ((wo_ref, wod_v.at[pl.ds(0, HEAD), :]), (wd_ref, wod_v.at[pl.ds(HEAD, FF), :]), (ao_ref, aod_v.at[:, pl.ds(0, HEAD), pl.ds(0, RANK)]), (ad_ref, aod_v.at[:, pl.ds(HEAD, FF), pl.ds(RANK, RANK)])),
     )
     copies = []
     n_sem = 0
@@ -65,7 +67,7 @@
     def xcopy(u):
         rows = pl.ds(pl.multiple_of(u * HALF, HALF), HALF)
         s = lax.rem(u, 2)
-        return pltpu.make_async_copy(h_ref.at[rows, :], hbuf.at[s], x_sem.at[s])
+        return pltpu.make_async_copy(x_ref.at[rows, :], xbuf.at[s], x_sem.at[s])
 
     CB = bown_ref.shape[-1]
 
@@ -73,7 +75,13 @@
         return pl.ds(pl.multiple_of(d * CB, CB), CB)
 
     bown = pltpu.make_async_copy(bown_ref, bod_v.at[:, :, bcols(idx)], loc_sem.at[2])
+    def arows(d):
+        return pl.ds(pl.multiple_of(d * AR, AR), AR)
+
+    aown = pltpu.make_async_copy(aown_ref, at_v.at[:, arows(idx), :], loc_sem.at[3])
+    aown.start()
     xcopy(0).start()
+    aod_v[...] = jnp.zeros_like(aod_v)
     for row in copies:
         for cp in row:
             cp.start()
@@ -88,7 +96,10 @@
     kbuf[...] = jnp.zeros_like(kbuf)
 
     def settle(t, hf, k):
-        if hf == 0:
+        if isinstance(t, int):
+            for cp in copies[k]:
+                cp.wait()
+        elif hf == 0 and k > 0:
             @pl.when(t == 0)
             def _():
                 for cp in copies[k]:
@@ -105,7 +116,7 @@
 
     def d2d(t):
         s = lax.rem(t, 2)
-        return rc(psend, l0.at[s], d2d_s, d2d_r.at[s], mate)
+        return tuple(rc(psend.at[:, cols], l0.at[s, :, cols], d2d_s.at[k], d2d_r.at[s, k], mate) for k, cols in enumerate((A, B)))
 
     def first_copies(src, q, rows, lf, ld, ss, rs, plus, minus):
         return (rc(src.at[blk(q, 2, rows), A], lf.at[0], ss.at[0], rs.at[0], plus),
@@ -252,18 +263,18 @@
 
     def e8(t):
         wrecv(agb2(t))
+        wsend(agb1(t))
+        wsend(aga2(t))
         start((dd(t),))
 
     def e9(t):
         wrecv((dd(t),))
         wsend((dd(t),))
         wsend(agb2(t))
-        wsend(agb1(t))
-        wsend(aga2(t))
 
     F32 = jnp.float32
 
-    def pa(t, hf):
+    def pn(t, hf):
         u = 2 * t + hf
         settle(t, hf, 0)
         xcopy(u).wait()
@@ -271,8 +282,26 @@
         @pl.when(u + 1 < 2 * NT)
         def _():
             xcopy(u + 1).start()
+        s = lax.rem(u, 2)
+        RB = 16
+
+        def step(k, _):
+            rows = pl.ds(pl.multiple_of(k * RB, RB), RB)
+            xf = xbuf[s, rows, :].astype(F32)
+            inv = lax.rsqrt(jnp.sum(xf * xf, axis=-1, keepdims=True) * (1.0 / D) + EPS)
+            hbuf[rows, :] = (xf * inv * gain_v[...]).astype(BF)
+            return 0
+        lax.fori_loop(0, HALF // RB, step, 0, unroll=8)
+
+    def nt(a, b):
+        return lax.dot_general(a, b, (((1,), (1,)), ((), ())), preferred_element_type=F32)
+
+    def pm(t, hf):
         i = ids_ref[t // tps]
-        mids[...] = lax.dot_general(hbuf[hf], at_v[i], (((1,), (1,)), ((), ())), preferred_element_type=F32).astype(BF)
+        n = at_v.shape[1]
+        both = at_v[pl.ds(2 * i, 2)].reshape(2 * n, D)
+        mids[:, pl.ds(0, 2 * n)] = nt(hbuf[...], both).astype(BF)
+        mids[:, pl.ds(2 * n, n)] = nt(hbuf[...], at_v[at_v.shape[0] - 1]).astype(BF)
 
     def rope(z, rows):
         return z * cos_v[rows, :] + pltpu.roll(z, HEAD // 2, 1) * sin_v[rows, :]
@@ -281,9 +310,10 @@
         settle(t, hf, 1)
         i = ids_ref[t // tps]
         pos = pl.ds(pl.multiple_of(lax.rem(t, tps) * TT + hf * HALF, HALF), HALF)
-        z = jnp.dot(hbuf[hf], wqkv_v[...], preferred_element_type=F32)
-        lqk = jnp.dot(mids[:, pl.ds(0, 2 * HEAD)], bqk_v[i], preferred_element_type=F32)
-        lv = jnp.dot(mids[:, pl.ds(2 * HEAD, 2 * HEAD)], bv_v[i], preferred_element_type=F32)
+        z = jnp.dot(hbuf[...], wqkv_v[...], preferred_element_type=F32)
+        n = at_v.shape[1]
+        lqk = jnp.dot(mids[:, pl.ds(0, n)], bin_v[i, :, pl.ds(0, 2 * HEAD)], preferred_element_type=F32)
+        lv = jnp.dot(mids[:, pl.ds(2 * n, n)], bin_v[i, :, pl.ds(2 * HEAD, HEAD)], preferred_element_type=F32)
         qbuf[...] = rope(z[:, :HEAD] + scale * lqk[:, :HEAD], pos).astype(BF)
         kbuf[pos, :] = rope(z[:, HEAD:2 * HEAD] + scale * lqk[:, HEAD:], pos).astype(BF)
         vbuf[pos, :] = (z[:, 2 * HEAD:] + scale * lv).astype(BF)
@@ -293,8 +323,8 @@
         i = ids_ref[t // tps]
         for n in range(FF // FB):
             cols = pl.ds(n * 2 * FB, 2 * FB)
-            z = jnp.dot(hbuf[hf], wgu_v[:, cols], preferred_element_type=F32)
-            z = z + scale * jnp.dot(mids[:, pl.ds(4 * HEAD, 2 * HEAD)], bgu_v[i, :, cols], preferred_element_type=F32)
+            z = jnp.dot(hbuf[...], wgu_v[:, cols], preferred_element_type=F32)
+            z = z + scale * jnp.dot(mids[:, pl.ds(at_v.shape[1], at_v.shape[1])], bin_v[i, :, pl.ds(3 * HEAD + n * 2 * FB, 2 * FB)], preferred_element_type=F32)
             g = z[:, :FB]
             om[lax.rem(t, 2), hf, :, pl.ds(HEAD + n * FB, FB)] = (g * (1.0 / (1.0 + jnp.exp(-g))) * z[:, FB:]).astype(BF)
 
@@ -307,16 +337,16 @@
         p = (e / jnp.sum(e, axis=-1, keepdims=True)).astype(BF)
         om[lax.rem(t, 2), hf, :, pl.ds(0, HEAD)] = jnp.dot(p, vbuf[...], preferred_element_type=F32).astype(BF)
 
-    def out_proj(t, half, dst, extra):
+    def out_proj(t, half, dst, extra, hooks):
         i = ids_ref[t // tps]
         act = om[lax.rem(t, 2), half]
-        last = jnp.dot(act, aod_v[i], preferred_element_type=F32)
-        tail = pl.ds(D, W - D)
-        dst[:, tail] = (last if extra is None else last + extra[:, tail].astype(F32)).astype(BF)
         NB = 512
-        for n in range(D // NB):
-            cols = pl.ds(n * NB, NB)
-            acc = jnp.dot(act, wod_v[:, cols], preferred_element_type=F32)
+        for n in range(D // NB + 1):
+            cols = pl.ds(n * NB, min(NB, W - n * NB))
+            if n in hooks:
+                hooks[n]()
+            w = wod_v[:, cols] if n < D // NB else aod_v[i]
+            acc = jnp.dot(act, w, preferred_element_type=F32)
             dst[:, cols] = (acc if extra is None else acc + extra[:, cols].astype(F32)).astype(BF)
 
     def pf(t):
@@ -324,14 +354,14 @@
 
         @pl.when(t >= 1)
         def _():
-            d2d(t - 1).wait_send()
-        out_proj(t, 1 - c, psend, None)
-        d2d(t).start()
+            wsend(d2d(t - 1))
+        out_proj(t, 1 - c, psend, None, {5: lambda: d2d(t)[0].start()})
+        d2d(t)[1].start()
 
     def pg(t):
-        d2d(t).wait_recv()
-        out_proj(t, c, r0, l0.at[lax.rem(t, 2)])
-        start(p1s1(t))
+        out_proj(t, c, r0, l0.at[lax.rem(t, 2)], {0: lambda: d2d(t)[0].wait_recv(), 4: lambda: d2d(t)[1].wait_recv(),
+                                                 5: lambda: start(p1s1(t)[0::3])})
+        start(p1s1(t)[1:3])
 
     def guard(t, f, *a):
         @pl.when(jnp.logical_and(t >= 0, t < NT))
@@ -390,46 +420,110 @@
         def _():
             f()
 
+    def ln(dev, r):
+        return dev - q2 * st2 + lax.rem(q2 + r + R, R) * st2
+
+    def arow(d, k, dev, cols):
+        ref = at_v.at[:, arows(d), cols]
+        return rc(ref, ref, ag_s.at[k], ag_r.at[k], dev)
+
+    full = pl.ds(0, D)
+    opp1 = base1 + lax.rem(q1 + 2, R) * st1
+    lines = (idx, minus1, plus1, opp1)
+
+    def a1():
+        return (arow(idx, 0, plus2, full), arow(idx, 1, minus2, full))
+
+    def a2():
+        return (arow(minus2, 2, plus2, DA), arow(plus2, 3, minus2, DB))
+
+    def ab(r):
+        return (arow(ln(idx, r), 4 + r % R, plus1, full), arow(ln(idx, r), 4 + R + r % R, minus1, full))
+
+    def af(r):
+        return (arow(ln(minus1, r), 4 + 2 * R + r % R, plus1, DA), arow(ln(plus1, r), 4 + 3 * R + r % R, minus1, DB))
+
+    def am(j, r):
+        return (arow(ln(lines[j], r), 4 + 4 * R + R * j + r % R, mate, full),)
+
+    def gather_a():
+        aown.wait()
+        start(a1())
+        start(ab(0))
+        start(am(0, 0))
+        pn(0, 0)
+        wrecv(a1())
+        start(a2())
+        for r in (-1, 1):
+            start(ab(r))
+            start(am(0, r))
+        wrecv(a2())
+        start(ab(2))
+        start(am(0, 2))
+        for r in (0, -1, 1, 2):
+            wrecv(ab(r))
+            start(af(r))
+            start(am(1, r))
+            start(am(2, r))
+        for r in (0, -1, 1, 2):
+            wrecv(af(r))
+            start(am(3, r))
+        for j in range(4):
+            for r in (0, -1, 1, 2):
+                wrecv(am(j, r))
+        wsend(a1())
+        wsend(a2())
+        for r in (0, -1, 1, 2):
+            wsend(ab(r))
+            wsend(af(r))
+            for j in range(4):
+                wsend(am(j, r))
+
+    gather_a()
     b1()
 
     def body(it, _):
-        guard(it, pa, 0)
+        at_step(it, 3, b6)
+        @pl.when(jnp.logical_and(it >= 1, it < NT))
+        def _():
+            pn(it, 0)
+        guard(it - 3, e4)
+        guard(it, pm, 0)
+        guard(it - 2, e2)
+        guard(it - 1, pg)
         guard(it, pb, 0)
         at_step(it, 0, b2)
         at_step(it, 1, b4)
-        at_step(it, 3, b6)
+        guard(it, pc, 0)
         guard(it - 5, e7)
-        guard(it - 4, e5)
-        guard(it - 3, e4)
-        guard(it - 2, e2)
-        guard(it - 1, pg)
-        guard(it, pc, 0)
         guard(it, pd, 0)
-        guard(it, pa, 1)
+        guard(it, pn, 1)
+        guard(it, pm, 1)
+        guard(it - 3, e5)
+        guard(it - 2, e3)
         guard(it, pb, 1)
+        guard(it - 1, e1)
         at_step(it, 0, b3)
         at_step(it, 1, b5)
-        guard(it - 1, e1)
-        guard(it - 2, e3)
-        guard(it - 4, e6)
-        guard(it - 5, e8)
-        guard(it - 6, e9)
         guard(it, pc, 1)
+        guard(it - 6, e8)
         guard(it, pd, 1)
+        guard(it - 3, e6)
         guard(it, pf)
+        guard(it - 7, e9)
         return 0
-    lax.fori_loop(0, NT + 6, body, 0)
+    lax.fori_loop(0, NT + 7, body, 0)
     last = NT - 1
-    d2d(last).wait_send()
+    wsend(d2d(last))
     wsend(p1s2(last))
     wsend(p2s2(last))
 
 
-def fused(mesh, ids, x, h, at, wq, wk, wv, wg, wu, wo, wd, bqk, bv, bgu, aod, bown, cos, sin, scale, seq_len, TT):
+def fused(mesh, ids, x, gain, aown, wq, wk, wv, wg, wu, wo, wd, b_in, ao, ad, bown, cos, sin, scale, seq_len, TT):
     R = math.isqrt(mesh.shape["tensor"] // 2)
     T, D = x.shape
     HEAD, FF = wo.shape[0], wd.shape[0]
-    W = D + aod.shape[-1]
+    W = D + 2 * ao.shape[-1]
     NT, HALF = T // TT, TT // 2
     B1 = HALF // R
     B2 = B1 // R
@@ -439,47 +533,23 @@
 
     def V(*shape):
         return pltpu.VMEM(shape, BF)
-    n_in = 17
+    n_in = 16
+    rows_a = aown.shape[1] * mesh.shape["tensor"]
     return pl.pallas_call(
         functools.partial(fused_kernel, cfg), name="block",
         out_shape=jax.ShapeDtypeStruct((T, D), BF),
         in_specs=[pl.BlockSpec(memory_space=pltpu.SMEM)] + [pl.BlockSpec(memory_space=pltpu.HBM)] * n_in,
         out_specs=pl.BlockSpec(memory_space=pltpu.HBM),
-        scratch_shapes=[V(2, HALF, D), V(HALF, at.shape[1]), V(*at.shape), V(D, 3 * HEAD), V(D, 2 * FF), V(HEAD + FF, D),
-                        V(*bqk.shape), V(*bv.shape), V(*bgu.shape), V(*aod.shape), V(*bown.shape[:2], D),
+        scratch_shapes=[V(2, HALF, D), V(HALF, D), V(HALF, 3 * rows_a), pltpu.VMEM(gain.shape, jnp.float32), V(aown.shape[0], rows_a, D), V(D, 3 * HEAD), V(D, 2 * FF), V(HEAD + FF, D),
+                        V(*b_in.shape), V(ao.shape[0], HEAD + FF, W - D), V(*bown.shape[:2], D),
                         pltpu.VMEM(cos.shape, jnp.float32), pltpu.VMEM(sin.shape, jnp.float32), V(HALF, HEAD), V(seq_len, HEAD), V(seq_len, HEAD), V(2, 2, HALF, HEAD + FF),
                         V(HALF, W), V(2, HALF, W), V(HALF, W),
                         V(2, B1, WH), V(2, B1, WH), V(2, B1, WH), V(2, B1, WH), V(2, B1, W),
                         V(2, 2, B2, WH), V(2, 2, B2, WH), V(2, 2, B2, WH), V(2, B2, WH), V(B2, W),
                         V(B2, D), V(B2, D),
-                        S((17,)), S((2,)), S, S((2,)), S((6,)), S((6,)), S((2, 6)), S((2, 6)), S((4, 4)), S((4, 4)), S((4, 4)), S((4, 4)), S((4,)), S((4,)), S((4 + 4 * R + R * R,)), S((4 + 4 * R + R * R,)), S((3,))],
+                        S((15,)), S((2,)), S((2,)), S((2, 2)), S((6,)), S((6,)), S((2, 6)), S((2, 6)), S((4, 4)), S((4, 4)), S((4, 4)), S((4, 4)), S((4,)), S((4,)), S((4 + 8 * R,)), S((4 + 8 * R,)), S((4 + 4 * R + R * R,)), S((4 + 4 * R + R * R,)), S((4,))],
         compiler_params=pltpu.CompilerParams(collective_id=0, has_side_effects=True, vmem_limit_bytes=67043328),
-    )(ids, x, h, at, wq, wk, wv, wg, wu, wo, wd, bqk, bv, bgu, aod, bown, cos, sin)
-
-
-def norm_kernel(x_ref, gain_ref, h_ref):
-    rows_per = 16
-    dim = x_ref.shape[1]
-
-    def step(k, _):
-        rows = pl.ds(pl.multiple_of(k * rows_per, rows_per), rows_per)
-        xf = x_ref[rows, :].astype(jnp.float32)
-        inv = lax.rsqrt(jnp.sum(xf * xf, axis=-1, keepdims=True) * (1.0 / dim) + EPS)
-        h_ref[rows, :] = (xf * inv * gain_ref[...]).astype(BF)
-        return 0
-    lax.fori_loop(0, x_ref.shape[0] // rows_per, step, 0, unroll=4)
-
-
-def norm(x, gain):
-    T, D = x.shape
-    rows = 256
-    return pl.pallas_call(
-        norm_kernel, name="norm", grid=(T // rows,),
-        out_shape=jax.ShapeDtypeStruct((T, D), BF),
-        in_specs=[pl.BlockSpec((rows, D), lambda i: (i, 0)), pl.BlockSpec((1, D), lambda i: (0, 0))],
-        out_specs=pl.BlockSpec((rows, D), lambda i: (i, 0)),
-        cost_estimate=pl.CostEstimate(flops=8000 * T * D // 1000 * 1000, bytes_accessed=4 * T * D, transcendentals=0),
-    )(x, gain)
+    )(ids, x, gain, aown, wq, wk, wv, wg, wu, wo, wd, b_in, ao, ad, bown, cos, sin)
 
 
 def solution(mesh):
@@ -501,44 +571,34 @@
         dim = x_blk.shape[2]
         n_ad = a_query.shape[0]
         zero_a = jnp.zeros_like(a_value)
-        mine = jnp.concatenate([a_query, a_key, a_value, zero_a, a_gate, a_up], axis=2)
-        mine = jnp.transpose(mine, (0, 2, 1)).reshape(n_ad * 3, -1, dim)
-        a_all = lax.all_gather(mine, 'tensor', axis=1, tiled=True)
-        a_all = a_all.reshape(n_ad, -1, dim)
+        part = rank // n_dev
+        cols = [st[i] for i in range(n_ad) for st in (a_query, a_key, a_gate, a_up)] + [a_value[i] for i in range(n_ad)]
+        mine = jnp.transpose(jnp.concatenate(cols, axis=1)).reshape(2 * n_ad + 1, 2 * part, dim)
         b_own = jnp.concatenate([b_out, b_down], axis=1)
-        x_flat = x_blk.reshape(-1, dim)
-        normed = norm(x_flat, norm_gain.reshape(1, dim))
-
-        def weave(b_first, b_second):
-            first = b_first.reshape(n_ad, n_dev, rank // n_dev, -1)
-            second = b_second.reshape(n_ad, n_dev, rank // n_dev, -1)
-            return first, second
-
-        def pair(b_first, b_second):
-            first, second = weave(b_first, b_second)
-            zf, zs = jnp.zeros_like(first), jnp.zeros_like(second)
-            rows = jnp.concatenate([jnp.concatenate([first, zs], axis=3), jnp.concatenate([zf, second], axis=3)], axis=2)
-            return rows.reshape(n_ad, 2 * rank, -1)
-
         head = w_query.shape[-1]
         ff = w_gate.shape[1]
         tile = seq_len // 2
         fb = tile // 2
-        bqk = pair(b_query, b_key)
-        bv_first, _ = weave(b_value, b_value)
-        bv = jnp.concatenate([bv_first, jnp.zeros_like(bv_first)], axis=2).reshape(n_ad, 2 * rank, -1)
-        bgu = pair(b_gate, b_up).reshape(n_ad, 2 * rank, 2, ff // fb, fb)
-        bgu = jnp.transpose(bgu, (0, 1, 3, 2, 4)).reshape(n_ad, 2 * rank, 2 * ff)
-        ao = a_out.reshape(n_ad, head, rank)
-        aod = jnp.concatenate([jnp.concatenate([ao, jnp.zeros_like(ao)], axis=2), jnp.concatenate([jnp.zeros_like(a_down), a_down], axis=2)], axis=1)
+
+        def rows(stack):
+            return stack.reshape(n_ad, n_dev, part, -1)
+
+        bq, bk, bvv, bg, bu = (rows(b) for b in (b_query, b_key, b_value, b_gate, b_up))
+        zq, zg = jnp.zeros_like(bq), jnp.zeros_like(bg[..., :fb])
+        which = jnp.arange(n_ad).reshape(n_ad, 1, 1, 1)
+        top, low = [bq, zq, jnp.where(which == 0, bvv, zq)], [zq, bk, jnp.where(which == 1, bvv, zq)]
+        for n in range(ff // fb):
+            top += [bg[..., n * fb:(n + 1) * fb], zg]
+            low += [zg, bu[..., n * fb:(n + 1) * fb]]
+        b_in = jnp.concatenate([jnp.concatenate(top, axis=3), jnp.concatenate(low, axis=3)], axis=2).reshape(n_ad, 2 * rank, -1)
         half = head // 2
-        inv_freq = ROPE_BASE ** (-jnp.arange(half, dtype=jnp.float32) / half)
-        angles = jnp.arange(seq_len, dtype=jnp.float32)[:, None] * inv_freq[None, :]
-        cos_t, sin_t = jnp.cos(angles), jnp.sin(angles)
-        cos_t = jnp.concatenate([cos_t, cos_t], axis=1)
-        sin_t = jnp.concatenate([-sin_t, sin_t], axis=1)
-        out = fused(mesh, adapter_ids, x_flat, normed, a_all, w_query.reshape(dim, head), w_key.reshape(dim, head), w_value.reshape(dim, head),
-                    w_gate, w_up, w_out.reshape(head, dim), w_down, bqk, bv, bgu, aod, b_own, cos_t, sin_t, scale, seq_len, tile)
+        inv_freq = np.float32(ROPE_BASE) ** (-np.arange(half, dtype=np.float32) / np.float32(half))
+        angles = np.arange(seq_len, dtype=np.float32)[:, None] * inv_freq[None, :]
+        cos_t, sin_t = np.cos(angles), np.sin(angles)
+        cos_t = jnp.asarray(np.concatenate([cos_t, cos_t], axis=1))
+        sin_t = jnp.asarray(np.concatenate([-sin_t, sin_t], axis=1))
+        out = fused(mesh, adapter_ids, x_blk.reshape(-1, dim), norm_gain.reshape(1, dim), mine, w_query.reshape(dim, head), w_key.reshape(dim, head), w_value.reshape(dim, head),
+                    w_gate, w_up, w_out.reshape(head, dim), w_down, b_in, a_out.reshape(n_ad, head, rank), a_down, b_own, cos_t, sin_t, scale, seq_len, tile)
         return out.reshape(x_blk.shape)
 
     return jax.shard_map(local_layer, mesh=mesh, in_specs=in_specs, out_specs=batch_spec, check_vma=False)

time: 650 us -> 512 us (0.79)
  Pallas kernels: 575 us -> 454 us
  between operations: 13.5 us -> 0.12 us
    pallas_call x1 -> x0, Pallas kernels: 66.5 us -> none  [norm(): pl.pallas_call(norm_kernel, name='norm', grid=(T // rows,), out_shape=jax...]
    pallas_call x1, Pallas kernels: 508 us -> 454 us  [fused(): pl.pallas_call(functools.partial(fused_kernel, cfg), name='block', out_sh...]
    unnamed x15 -> x14, local copies, waits for them, and re-layouts: 44.5 us -> 45.8 us
  transfers between devices with their start and end apart: 1 -> 0, of which waited for: 0 -> 0; matrix products, arithmetic and copies ran while one was open for 2% -> 0% of each run, Pallas kernels for 10% -> 0%
where the time goes in v3:
time: 512 us
  Pallas kernels  454 us (89%)
  local copies, waits for them, and re-layouts  53.9 us (11%)
    pallas_call x1, Pallas kernels, fused(): pl.pallas_call(functools.partial(fused_kernel, cfg), name='block', out_sh...  454 us
    unnamed x14, local copies, waits for them, and re-layouts  45.8 us

profile of v3, /device:TPU:97, one launch (start us, length us, event | category | flops | bytes accessed | tf_op | source)
XLA Modules:
  0.0 512.0 jit_solution(3230789239355638625)
XLA Ops:
  0.0 0.0 copy-start
  0.0 0.0 copy-start.1
  0.0 0.8 slice_bitcast_fusion.5
  0.9 1.5 pad_maximum_fusion.bown_ref
  2.4 0.9 slice_bitcast_fusion.3
  3.3 0.9 slice_bitcast_fusion
  4.1 3.4 concatenate.15
  7.5 1.0 reshape.65
  8.5 1.0 reshape.67
  9.5 0.9 constant_dynamic-update-slice_fusion
  10.5 0.0 copy-done.1
  10.6 0.0 copy-done
  10.6 0.2 select_dynamic-update-slice_fusion.1
  10.7 0.1 slice_dynamic-update-slice_fusion.3
  10.9 0.1 broadcast_dynamic-update-slice_fusion
  10.9 0.1 slice_dynamic-update-slice_fusion.2
  11.0 0.1 broadcast_dynamic-update-slice_fusion.3
  11.1 0.1 slice_dynamic-update-slice_fusion.1
  11.1 0.1 broadcast_dynamic-update-slice_fusion.2
  11.2 0.1 slice_dynamic-update-slice_fusion
  11.3 1.8 maximum_bitcast_fusion.bin_ref
  13.1 454.4 %block.1 = bf16[8192,4096]{1,0:T(8,128)(2,1)} custom-call(s32[8]{0:T(128)} %ids_ref.1, bf16[8192,4096]{1,0:T(8,128)(2,1)} %bitcast.x_ref, f32[1,4096]{1,0:T(1,128)} %bitcast.45, bf16[5,8,4096]{2,1,0:T(8,128)(2,1)} %bitcast.36, bf16[4096,128]{1,0:T(8,128)(2,1)} %bitcast.37, bf16[4096,128]{1,0:T(8,128)(2,1)} %bitcast.38, bf16[4096,128]{1,0:T(8,128)(2,1)} %bitcast.39, ...), custom_call_target="tpu_custom_call" | custom-call | tf_op jit(solution)/shard_map/block/pallas_call | solution.py:538
  467.5 44.5 %copy.40 = bf16[8,1024,4096]{2,1,0:T(8,128)(2,1)} copy(bf16[8,1024,4096]{2,1,0:T(8,128)(2,1)} %bitcast.23) | data formatting | bytes 134217728
  (5 shorter events, 0.1 us)
Async XLA Ops:
  0.0 10.6 %copy-start = (bf16[2,128,1,128]{3,1,2,0:T(8,128)(2,1)S(1)}, bf16[2,128,1,128]{3,1,2,0:T(8,128)(2,1)}, u32[]{:S(2)}) copy-start(bf16[2,128,1,128]{3,1,2,0:T(8,128)(2,1)} %param.41) | copy-start | bytes 196612
  0.0 10.5 %copy-start.1 = (bf16[2,128,1,128]{3,1,2,0:T(8,128)(2,1)S(1)}, bf16[2,128,1,128]{3,1,2,0:T(8,128)(2,1)}, u32[]{:S(2)}) copy-start(bf16[2,128,1,128]{3,1,2,0:T(8,128)(2,1)} %param.39) | copy-start | bytes 196612

commit v4 on v3

--- a/solution.py
+++ b/solution.py
@@ -15,9 +15,9 @@
 MESH = pl.DeviceIdType.MESH
 BF = jnp.bfloat16
 
-def fused_kernel(cfg, ids_ref, x_ref, gain_ref, aown_ref, wq_ref, wk_ref, wv_ref, wg_ref, wu_ref, wo_ref, wd_ref, bin_ref, ao_ref, ad_ref,
-                 bown_ref, cos_ref, sin_ref, stage_ref,
-                 xbuf, hbuf, mids, gain_v, at_v, wqkv_v, wgu_v, wod_v, bin_v, aod_v, bod_v, cos_v, sin_v, qbuf, kbuf, vbuf, om,
+def fused_kernel(cfg, ids_ref, x_ref, gain_ref, aown_ref, avown_ref, wq_ref, wk_ref, wv_ref, wg_ref, wu_ref, wo_ref, wd_ref, bq_ref, bk_ref, bv_ref, bg_ref, bu_ref, ao_ref, ad_ref,
+                 bo_ref, bd_ref, cos_ref, sin_ref, stage_ref,
+                 xbuf, hbuf, mids, gain_v, at_v, wqkv_v, wgu_v, wod_v, bst_v, bin_v, aod_v, bod_v, cos_v, sin_v, qbuf, kbuf, vbuf, om,
                  psend, l0, r0, l1f, l1d, l1s, s1, r1, l2f, l2d, l2s, s2, r2, xrow, yrow,
                  w_sem, x_sem, d2d_s, d2d_r, p1_s, p1_r, p2_s, p2_r, aga_s, aga_r, agb_s, agb_r, dd_s, dd_r, ag_s, ag_r, bg_s, bg_r, loc_sem):
     R, NT, TT, W, D, HEAD, FF, scale, tps = cfg
@@ -50,7 +50,7 @@
     resident = (
         ((gain_ref, gain_v),),
         ((wq_ref, wqkv_v.at[:, pl.ds(0, HEAD)]), (wk_ref, wqkv_v.at[:, pl.ds(HEAD, HEAD)]), (wv_ref, wqkv_v.at[:, pl.ds(2 * HEAD, HEAD)]),
-         (bin_ref, bin_v), (cos_ref, cos_v), (sin_ref, sin_v)),
+         (cos_ref, cos_v), (sin_ref, sin_v)),
         ((wg_ref.at[:, pl.ds(0, FB)], wgu_v.at[:, pl.ds(0, FB)]), (wu_ref.at[:, pl.ds(0, FB)], wgu_v.at[:, pl.ds(FB, FB)]),
          (wg_ref.at[:, pl.ds(FB, FB)], wgu_v.at[:, pl.ds(2 * FB, FB)]), (wu_ref.at[:, pl.ds(FB, FB)], wgu_v.at[:, pl.ds(3 * FB, FB)])),
         ((wo_ref, wod_v.at[pl.ds(0, HEAD), :]), (wd_ref, wod_v.at[pl.ds(HEAD, FF), :]), (ao_ref, aod_v.at[:, pl.ds(0, HEAD), pl.ds(0, RANK)]), (ad_ref, aod_v.at[:, pl.ds(HEAD, FF), pl.ds(RANK, RANK)])),
@@ -69,24 +69,35 @@
         s = lax.rem(u, 2)
         return pltpu.make_async_copy(x_ref.at[rows, :], xbuf.at[s], x_sem.at[s])
 
-    CB = bown_ref.shape[-1]
+    CB = bo_ref.shape[-1]
 
     def bcols(d):
         return pl.ds(pl.multiple_of(d * CB, CB), CB)
 
-    bown = pltpu.make_async_copy(bown_ref, bod_v.at[:, :, bcols(idx)], loc_sem.at[2])
+    bown = tuple(pltpu.make_async_copy(ref, bod_v.at[:, pl.ds(k * RANK, RANK), bcols(idx)], loc_sem.at[2 + k]) for k, ref in enumerate((bo_ref, bd_ref)))
     def arows(d):
         return pl.ds(pl.multiple_of(d * AR, AR), AR)
 
-    aown = pltpu.make_async_copy(aown_ref, at_v.at[:, arows(idx), :], loc_sem.at[3])
-    aown.start()
+    n_qk = aown_ref.shape[0]
+    aown = (pltpu.make_async_copy(aown_ref, at_v.at[pl.ds(0, n_qk), arows(idx), :], loc_sem.at[4]),
+            pltpu.make_async_copy(avown_ref, at_v.at[pl.ds(n_qk, 1), arows(idx), :], loc_sem.at[5]))
+    for cp in aown:
+        cp.start()
+    bcol = [(bq_ref, 0, HEAD, 0, 0), (bk_ref, HEAD, HEAD, 0, 1), (bv_ref, 2 * HEAD, HEAD, 0, 2)]
+    for n in range(FF // FB):
+        bcol += [(bg_ref, 3 * HEAD + 2 * n * FB, FB, n * FB, 0), (bu_ref, 3 * HEAD + (2 * n + 1) * FB, FB, n * FB, 1)]
+    bload = [pltpu.make_async_copy(ref.at[:, :, pl.ds(at, width)], bst_v.at[:, :, pl.ds(col, width)], loc_sem.at[6 + k])
+             for k, (ref, col, width, at, _) in enumerate(bcol)]
+    for cp in bload:
+        cp.start()
     xcopy(0).start()
     aod_v[...] = jnp.zeros_like(aod_v)
     for row in copies:
         for cp in row:
             cp.start()
 
-    bown.start()
+    for cp in bown:
+        cp.start()
 
     bar = pltpu.get_barrier_semaphore()
     for p in peers:
@@ -155,7 +166,7 @@
         return rc(stage_ref.at[rows, cols], stage_ref.at[rows, cols], ss, rs, dev)
 
     def sl(t):
-        return lax.rem(t, 4)
+        return lax.rem(t, 8)
 
     def aga1(t):
         s, r = sl(t), rows_a(t, 0)
@@ -167,19 +178,20 @@
         return (same(rows_a(t, -1), DA, aga_s.at[s, 2], aga_r.at[s, 2], plus2),
                 same(rows_a(t, 1), DB, aga_s.at[s, 3], aga_r.at[s, 3], minus2))
 
-    def agb1(t):
-        s, r = sl(t), rows_b(t, 0)
-        return (same(r, pl.ds(0, D), agb_s.at[s, 0], agb_r.at[s, 0], plus1),
-                same(r, pl.ds(0, D), agb_s.at[s, 1], agb_r.at[s, 1], minus1))
+    def agb1(t, r):
+        s, rows, k = sl(t), rows_a(t, r), 2 * (r % R)
+        src = yrow if r == 0 else stage_ref.at[rows, :]
+        return (rc(src, stage_ref.at[rows, :], agb_s.at[s, k], agb_r.at[s, k], plus1),
+                rc(src, stage_ref.at[rows, :], agb_s.at[s, k + 1], agb_r.at[s, k + 1], minus1))
 
     def agb2(t):
         s = sl(t)
-        return (same(rows_b(t, -1), DA, agb_s.at[s, 2], agb_r.at[s, 2], plus1),
-                same(rows_b(t, 1), DB, agb_s.at[s, 3], agb_r.at[s, 3], minus1))
-
-    def dd(t):
-        s, r = sl(t), pl.ds(pl.multiple_of(row0(t), HALF), HALF)
-        return same(r, pl.ds(0, D), dd_s.at[s], dd_r.at[s], mate)
+        return (same(rows_b(t, -1), DA, agb_s.at[s, 8], agb_r.at[s, 8], plus1),
+                same(rows_b(t, 1), DB, agb_s.at[s, 9], agb_r.at[s, 9], minus1))
+
+    def dd(t, r):
+        s, k = lax.rem(t, 8), r % R
+        return (same(rows_b(t, r), pl.ds(0, D), dd_s.at[s, k], dd_r.at[s, k], mate),)
 
     def yloc(t):
         return pltpu.make_async_copy(yrow, stage_ref.at[rows_a(t, 0), :], loc_sem.at[0])
@@ -246,30 +258,40 @@
         yrow[...] = y.astype(BF)
         yloc(t).start()
         start(aga1(t))
+        start(agb1(t, 0))
 
     def e5(t):
         yloc(t).wait()
         wsend(aga1(t))
+        wsend(agb1(t, 0))
         wrecv(aga1(t))
         start(aga2(t))
+        start(agb1(t, -1))
+        start(agb1(t, 1))
 
     def e6(t):
         wrecv(aga2(t))
-        start(agb1(t))
+        start(agb1(t, 2))
+        start(dd(t, 0))
 
     def e7(t):
-        wrecv(agb1(t))
+        for r in (0, -1, 1, 2):
+            wrecv(agb1(t, r))
         start(agb2(t))
+        start(dd(t, -1))
+        start(dd(t, 1))
+        for r in (-1, 1, 2):
+            wsend(agb1(t, r))
+        wsend(aga2(t))
 
     def e8(t):
         wrecv(agb2(t))
-        wsend(agb1(t))
-        wsend(aga2(t))
-        start((dd(t),))
+        start(dd(t, 2))
 
     def e9(t):
-        wrecv((dd(t),))
-        wsend((dd(t),))
+        for r in (0, -1, 1, 2):
+            wrecv(dd(t, r))
+            wsend(dd(t, r))
         wsend(agb2(t))
 
     F32 = jnp.float32
@@ -391,7 +413,8 @@
         return tuple(piece(None, 2 * j + c, 4 + 4 * R + j, mate) for j in range(R * R))
 
     def b1():
-        bown.wait()
+        for cp in bown:
+            cp.wait()
         start(g1())
 
     def b2():
@@ -446,8 +469,22 @@
     def am(j, r):
         return (arow(ln(lines[j], r), 4 + 4 * R + R * j + r % R, mate, full),)
 
+    def weave():
+        for cp in bload:
+            cp.wait()
+        n = bin_v.shape[1]
+        part = AR // 2
+        row = lax.broadcasted_iota(jnp.int32, (n, RANK), 0)
+        col = lax.broadcasted_iota(jnp.int32, (n, RANK), 1)
+        picks = [jnp.where(row == (col // part) * AR + part * k + lax.rem(col, part), 1.0, 0.0).astype(BF) for k in range(2)]
+        for ad in range(bin_v.shape[0]):
+            for _, at, width, _, kind in bcol:
+                pick = picks[ad if kind == 2 else kind]
+                bin_v[ad, :, pl.ds(at, width)] = jnp.dot(pick, bst_v[ad, :, pl.ds(at, width)], preferred_element_type=F32).astype(BF)
+
     def gather_a():
-        aown.wait()
+        for cp in aown:
+            cp.wait()
         start(a1())
         start(ab(0))
         start(am(0, 0))
@@ -460,6 +497,7 @@
         wrecv(a2())
         start(ab(2))
         start(am(0, 2))
+        weave()
         for r in (0, -1, 1, 2):
             wrecv(ab(r))
             start(af(r))
@@ -484,42 +522,42 @@
 
     def body(it, _):
         at_step(it, 3, b6)
+        guard(it - 3, e4)
+        guard(it - 8, e9)
         @pl.when(jnp.logical_and(it >= 1, it < NT))
         def _():
             pn(it, 0)
-        guard(it - 3, e4)
+        guard(it - 2, e2)
         guard(it, pm, 0)
-        guard(it - 2, e2)
         guard(it - 1, pg)
-        guard(it, pb, 0)
         at_step(it, 0, b2)
         at_step(it, 1, b4)
+        guard(it, pb, 0)
+        guard(it - 3, e5)
         guard(it, pc, 0)
-        guard(it - 5, e7)
+        guard(it - 7, e8)
         guard(it, pd, 0)
         guard(it, pn, 1)
         guard(it, pm, 1)
-        guard(it - 3, e5)
         guard(it - 2, e3)
         guard(it, pb, 1)
         guard(it - 1, e1)
+        guard(it - 5, e7)
         at_step(it, 0, b3)
         at_step(it, 1, b5)
         guard(it, pc, 1)
-        guard(it - 6, e8)
+        guard(it - 3, e6)
         guard(it, pd, 1)
-        guard(it - 3, e6)
         guard(it, pf)
-        guard(it - 7, e9)
         return 0
-    lax.fori_loop(0, NT + 7, body, 0)
+    lax.fori_loop(0, NT + 8, body, 0)
     last = NT - 1
     wsend(d2d(last))
     wsend(p1s2(last))
     wsend(p2s2(last))
 
 
-def fused(mesh, ids, x, gain, aown, wq, wk, wv, wg, wu, wo, wd, b_in, ao, ad, bown, cos, sin, scale, seq_len, TT):
+def fused(mesh, ids, x, gain, aown, avown, wq, wk, wv, wg, wu, wo, wd, bq, bk, bv, bg, bu, ao, ad, bo, bd, cos, sin, scale, seq_len, TT):
     R = math.isqrt(mesh.shape["tensor"] // 2)
     T, D = x.shape
     HEAD, FF = wo.shape[0], wd.shape[0]
@@ -533,23 +571,25 @@
 
     def V(*shape):
         return pltpu.VMEM(shape, BF)
-    n_in = 16
+    n_in = 22
+    n_ad, rank = bq.shape[:2]
+    b_cols = 3 * HEAD + 2 * FF
     rows_a = aown.shape[1] * mesh.shape["tensor"]
     return pl.pallas_call(
         functools.partial(fused_kernel, cfg), name="block",
         out_shape=jax.ShapeDtypeStruct((T, D), BF),
         in_specs=[pl.BlockSpec(memory_space=pltpu.SMEM)] + [pl.BlockSpec(memory_space=pltpu.HBM)] * n_in,
         out_specs=pl.BlockSpec(memory_space=pltpu.HBM),
-        scratch_shapes=[V(2, HALF, D), V(HALF, D), V(HALF, 3 * rows_a), pltpu.VMEM(gain.shape, jnp.float32), V(aown.shape[0], rows_a, D), V(D, 3 * HEAD), V(D, 2 * FF), V(HEAD + FF, D),
-                        V(*b_in.shape), V(ao.shape[0], HEAD + FF, W - D), V(*bown.shape[:2], D),
+        scratch_shapes=[V(2, HALF, D), V(HALF, D), V(HALF, 3 * rows_a), pltpu.VMEM(gain.shape, jnp.float32), V(aown.shape[0] + 1, rows_a, D), V(D, 3 * HEAD), V(D, 2 * FF), V(HEAD + FF, D),
+                        V(n_ad, rank, b_cols), V(n_ad, rows_a, b_cols), V(ao.shape[0], HEAD + FF, W - D), V(bo.shape[0], W - D, D),
                         pltpu.VMEM(cos.shape, jnp.float32), pltpu.VMEM(sin.shape, jnp.float32), V(HALF, HEAD), V(seq_len, HEAD), V(seq_len, HEAD), V(2, 2, HALF, HEAD + FF),
                         V(HALF, W), V(2, HALF, W), V(HALF, W),
                         V(2, B1, WH), V(2, B1, WH), V(2, B1, WH), V(2, B1, WH), V(2, B1, W),
                         V(2, 2, B2, WH), V(2, 2, B2, WH), V(2, 2, B2, WH), V(2, B2, WH), V(B2, W),
                         V(B2, D), V(B2, D),
-                        S((15,)), S((2,)), S((2,)), S((2, 2)), S((6,)), S((6,)), S((2, 6)), S((2, 6)), S((4, 4)), S((4, 4)), S((4, 4)), S((4, 4)), S((4,)), S((4,)), S((4 + 8 * R,)), S((4 + 8 * R,)), S((4 + 4 * R + R * R,)), S((4 + 4 * R + R * R,)), S((4,))],
+                        S((14,)), S((2,)), S((2,)), S((2, 2)), S((6,)), S((6,)), S((2, 6)), S((2, 6)), S((8, 4)), S((8, 4)), S((8, 10)), S((8, 10)), S((8, 4)), S((8, 4)), S((4 + 8 * R,)), S((4 + 8 * R,)), S((4 + 4 * R + R * R,)), S((4 + 4 * R + R * R,)), S((6 + 3 + 2 * (2 * FF // TT),))],
         compiler_params=pltpu.CompilerParams(collective_id=0, has_side_effects=True, vmem_limit_bytes=67043328),
-    )(ids, x, gain, aown, wq, wk, wv, wg, wu, wo, wd, b_in, ao, ad, bown, cos, sin)
+    )(ids, x, gain, aown, avown, wq, wk, wv, wg, wu, wo, wd, bq, bk, bv, bg, bu, ao, ad, bo, bd, cos, sin)
 
 
 def solution(mesh):
@@ -567,38 +607,26 @@
         seq_len = x_blk.shape[1]
         rank = a_out.shape[-1]
         scale = ALPHA / rank
-        n_dev = mesh.shape['tensor']
         dim = x_blk.shape[2]
         n_ad = a_query.shape[0]
         zero_a = jnp.zeros_like(a_value)
-        part = rank // n_dev
-        cols = [st[i] for i in range(n_ad) for st in (a_query, a_key, a_gate, a_up)] + [a_value[i] for i in range(n_ad)]
-        mine = jnp.transpose(jnp.concatenate(cols, axis=1)).reshape(2 * n_ad + 1, 2 * part, dim)
-        b_own = jnp.concatenate([b_out, b_down], axis=1)
+        by_rank = [jnp.transpose(st, (0, 2, 1)) for st in (a_query, a_key, a_gate, a_up)]
+        mine = jnp.concatenate(by_rank, axis=1).reshape(2 * n_ad, -1, dim)
+        mine_v = jnp.transpose(a_value, (0, 2, 1)).reshape(1, -1, dim)
         head = w_query.shape[-1]
-        ff = w_gate.shape[1]
         tile = seq_len // 2
-        fb = tile // 2
-
-        def rows(stack):
-            return stack.reshape(n_ad, n_dev, part, -1)
-
-        bq, bk, bvv, bg, bu = (rows(b) for b in (b_query, b_key, b_value, b_gate, b_up))
-        zq, zg = jnp.zeros_like(bq), jnp.zeros_like(bg[..., :fb])
-        which = jnp.arange(n_ad).reshape(n_ad, 1, 1, 1)
-        top, low = [bq, zq, jnp.where(which == 0, bvv, zq)], [zq, bk, jnp.where(which == 1, bvv, zq)]
-        for n in range(ff // fb):
-            top += [bg[..., n * fb:(n + 1) * fb], zg]
-            low += [zg, bu[..., n * fb:(n + 1) * fb]]
-        b_in = jnp.concatenate([jnp.concatenate(top, axis=3), jnp.concatenate(low, axis=3)], axis=2).reshape(n_ad, 2 * rank, -1)
+
+        def flat(b_stack):
+            return b_stack.reshape(n_ad, rank, head)
+
         half = head // 2
         inv_freq = np.float32(ROPE_BASE) ** (-np.arange(half, dtype=np.float32) / np.float32(half))
         angles = np.arange(seq_len, dtype=np.float32)[:, None] * inv_freq[None, :]
         cos_t, sin_t = np.cos(angles), np.sin(angles)
         cos_t = jnp.asarray(np.concatenate([cos_t, cos_t], axis=1))
         sin_t = jnp.asarray(np.concatenate([-sin_t, sin_t], axis=1))
-        out = fused(mesh, adapter_ids, x_blk.reshape(-1, dim), norm_gain.reshape(1, dim), mine, w_query.reshape(dim, head), w_key.reshape(dim, head), w_value.reshape(dim, head),
-                    w_gate, w_up, w_out.reshape(head, dim), w_down, b_in, a_out.reshape(n_ad, head, rank), a_down, b_own, cos_t, sin_t, scale, seq_len, tile)
+        out = fused(mesh, adapter_ids, x_blk.reshape(-1, dim), norm_gain.reshape(1, dim), mine, mine_v, w_query.reshape(dim, head), w_key.reshape(dim, head), w_value.reshape(dim, head),
+                    w_gate, w_up, w_out.reshape(head, dim), w_down, flat(b_query), flat(b_key), flat(b_value), b_gate, b_up, a_out.reshape(n_ad, head, rank), a_down, b_out, b_down, cos_t, sin_t, scale, seq_len, tile)
         return out.reshape(x_blk.shape)
 
     return jax.shard_map(local_layer, mesh=mesh, in_specs=in_specs, out_specs=batch_spec, check_vma=False)

time: 512 us -> 496 us (0.969)
  local copies, waits for them, and re-layouts: 53.9 us -> 46 us
  Pallas kernels: 454 us -> 448 us
    pallas_call x1, Pallas kernels: 454 us -> 448 us  [fused(): pl.pallas_call(functools.partial(fused_kernel, cfg), name='block', out_sh...]
    unnamed x14 -> x1, local copies, waits for them, and re-layouts: 45.8 us -> 44.5 us
where the time goes in v4:
time: 496 us
  Pallas kernels  448 us (90%)
  local copies, waits for them, and re-layouts  46 us (9%)
    pallas_call x1, Pallas kernels, fused(): pl.pallas_call(functools.partial(fused_kernel, cfg), name='block', out_sh...  448 us
    unnamed x1, local copies, waits for them, and re-layouts  44.5 us

profile of v4, /device:TPU:97, one launch (start us, length us, event | category | flops | bytes accessed | tf_op | source)
XLA Modules:
  0.0 496.0 jit_solution(5621257878432701066)
XLA Ops:
  0.0 1.5 reshape.42.avown_ref
  1.5 1.8 pad_maximum_fusion
  3.3 448.2 %block.1 = bf16[8192,4096]{1,0:T(8,128)(2,1)} custom-call(s32[8]{0:T(128)} %ids_ref.1, bf16[8192,4096]{1,0:T(8,128)(2,1)} %bitcast.x_ref, f32[1,4096]{1,0:T(1,128)} %bitcast.31, bf16[4,8,4096]{2,1,0:T(8,128)(2,1)} %bitcast.21, bf16[1,8,4096]{2,1,0:T(8,128)(2,1)} %reshape.42.avown_ref, bf16[4096,128]{1,0:T(8,128)(2,1)} %bitcast.17, ...), custom_call_target="tpu_custom_call" | custom-call | tf_op jit(solution)/shard_map/block/pallas_call | solution.py:578
  451.5 44.5 %copy.28 = bf16[8,1024,4096]{2,1,0:T(8,128)(2,1)} copy(bf16[8,1024,4096]{2,1,0:T(8,128)(2,1)} %bitcast.16) | data formatting | bytes 134217728
